TPU v7x, 32 devices: a whole 2x2x4 slice. The times are simulated.
32 devices in a mesh: gp: 2 (over x), blk: 16 (over z, y, core).
Axes of the slice: x: 2, y: 2, z: 4, core: 2. Of those that a mesh axis runs over, the one named last changes fastest.
Arguments:
- points: float32 [8, 8192], P(None, ('gp', 'blk')), parts along dimension 1, may hold values from -6 to 6
- vectors: float32 [8, 8192], P(None, ('gp', 'blk')), parts along dimension 1, may hold values from -6 to 6
- inv_length: float32 [16], P('gp'), parts along dimension 0, may hold values from 0.15 to 0.6
- noise: float32 [2], P('gp'), parts along dimension 0, may hold values from 0.1 to 1
Outputs:
- product: float32 [8, 8192], P(None, ('gp', 'blk')), parts along dimension 1
There are 2 independent parts, one for each index of `gp`. A program takes and returns all parts, laid end to end along the dimension named above; each array names one. Nothing has to cross between parts.
All inputs are finite; a program needn't handle non-finite values.
Results may differ from a plain program's by a relative error of at most 0.00017.
Values sent between devices are 32-bit elements; how exact they have to be, the bound alone decides.
No kernel may reach another device: no remote copies, remote signals or barrier semaphores. Data moves between devices by JAX's collectives and lax.ppermute only.
A program may use at most 64 MiB of HBM per device.

v0:
```python
import jax
import jax.numpy as jnp
from jax import lax
from jax.sharding import PartitionSpec as P


def matern(left, right, inv_length):
    scaled_left = left * inv_length[:, None]
    scaled_right = right * inv_length[:, None]
    sq_left = jnp.sum(scaled_left * scaled_left, axis=0)
    sq_right = jnp.sum(scaled_right * scaled_right, axis=0)
    cross = jnp.dot(
        scaled_left.T,
        scaled_right,
        precision=lax.Precision.HIGHEST,
        preferred_element_type=jnp.float32,
    )
    dist2 = jnp.maximum(sq_left[:, None] + sq_right[None, :] - 2.0 * cross, 0.0)
    scaled_dist = jnp.sqrt(5.0 * dist2)
    return (1.0 + scaled_dist + scaled_dist * scaled_dist / 3.0) * jnp.exp(-scaled_dist)


def apply_tile(vec_other, tile):
    return jnp.dot(
        vec_other, tile, precision=lax.Precision.HIGHEST, preferred_element_type=jnp.float32
    )


def on_device(points, vectors, inv_length, noise):
    count = lax.axis_size("blk")
    total_points = points.shape[1] * count
    tile = matern(lax.all_gather(points, "blk", axis=1, tiled=True), points, inv_length)
    own_sum = apply_tile(lax.all_gather(vectors, "blk", axis=1, tiled=True), tile)
    return noise[0] * vectors + own_sum / jnp.sqrt(jnp.float32(total_points))


def solution(mesh):
    return jax.shard_map(
        on_device,
        mesh=mesh,
        in_specs=(P(None, ("gp", "blk")), P(None, ("gp", "blk")), P("gp"), P("gp")),
        out_specs=P(None, ("gp", "blk")),
        check_vma=False,
    )
```

profile of v0, /device:TPU:0, one launch (start us, length us, event | category | flops | bytes accessed | tf_op | source)
XLA Modules:
  0.0 53.8 jit_solution(1640502386650977833)
XLA Ops:
  0.0 0.0 copy-start
  0.0 23.8 %all_gather.6 = f32[8,4096]{1,0:T(8,128)S(1)} all-gather(f32[8,256]{1,0:T(8,128)} %param.4), channel_id=1, replica_groups=mesh['gp'=2,'blk'=16] {'blk'}, dimensions={1}, use_global_device_ids=true | all-gather | bytes 139264 | tf_op jit(solution)/shard_map/all_gather | solution.py:32
  23.8 0.8 %multiply_reduce_fusion = f32[4096]{0:T(1024)S(1)} fusion(f32[8,4096]{1,0:T(8,128)S(1)} %all_gather.6, f32[8]{0:T(128)} %param.6), kind=kLoop, calls=%fused_computation.18 | loop fusion | flops 94208 | bytes 147488 | tf_op jit(solution)/shard_map/reduce_sum | solution.py:10
  24.6 0.8 %multiply_reduce_fusion.1 = f32[256]{0:T(256)S(1)} fusion(f32[8,256]{1,0:T(8,128)} %param.4, f32[8]{0:T(128)} %param.6), kind=kLoop, calls=%fused_computation.21 | loop fusion | flops 5888 | bytes 9248 | tf_op jit(solution)/shard_map/reduce_sum | solution.py:11
  25.4 6.4 %fusion.3 = f32[4096,256]{1,0:T(8,128)S(1)} fusion(f32[256]{0:T(256)S(1)} %multiply_reduce_fusion.1, f32[4096]{0:T(1024)S(1)} %multiply_reduce_fusion, f32[8,4096]{1,0:T(8,128)S(1)} %all_gather.6, f32[8]{0:T(128)} %param.6, f32[8,256]{1,0:T(8,128)} %param.4), kind=kOutput, calls=%fused_computation.4 | convolution fusion | flops 105940992 | bytes 4351008 | tf_op jit(solution)/shard_map/dot_general | solution.py:12
  31.8 0.0 copy-done
  31.8 17.8 %all_gather.7 = f32[8,4096]{1,0:T(8,128)S(1)} all-gather(f32[8,256]{1,0:T(8,128)S(1)} %copy-done), channel_id=1, replica_groups=mesh['gp'=2,'blk'=16] {'blk'}, dimensions={1}, use_global_device_ids=true | all-gather | bytes 139264 | tf_op jit(solution)/shard_map/all_gather | solution.py:33
  50.3 3.6 %fusion.20 = f32[8,256]{1,0:T(8,128)} fusion(f32[8,4096]{1,0:T(8,128)S(1)} %all_gather.7, f32[4096,256]{1,0:T(8,128)S(1)} %fusion.3, f32[8,256]{1,0:T(8,128)S(1)} %copy-done, f32[]{:T(128)} %bitcast.6), kind=kOutput, calls=%fused_computation.17 | convolution fusion | flops 106960896 | bytes 4341764 | tf_op jit(solution)/shard_map/dot_general | solution.py:24
Async XLA Ops:
  0.0 31.8 %copy-start = (f32[8,256]{1,0:T(8,128)S(1)}, f32[8,256]{1,0:T(8,128)}, u32[]{:S(2)}) copy-start(f32[8,256]{1,0:T(8,128)} %param.5) | copy-start | bytes 24580
where the time goes:
time: 54.1 us; the launch traced here: 53.8 us
  blocking collectives  41.6 us (77%)
  matrix products  9.97 us (18%)
  other arithmetic  1.55 us (3%)
  between operations  0.67 us (1%)
    all_gather x1, blocking collectives, on_device(): lax.all_gather(points, 'blk', axis=1, tiled=True)  23.8 us
    all_gather x1, blocking collectives, on_device(): lax.all_gather(vectors, 'blk', axis=1, tiled=True)  17.8 us
    dot_general x1, matrix products, matern(): jnp.dot(scaled_left.T, scaled_right, precision=lax.Precision.HIGHEST, pre...  6.41 us
    dot_general x1, matrix products, apply_tile(): jnp.dot(vec_other, tile, precision=lax.Precision.HIGHEST, preferred_eleme...  3.57 us

commit v1 on v0

v1 whole, which is shorter than its diff:
```python
import functools
import math

import jax
import jax.numpy as jnp
from jax import lax
from jax.experimental import pallas as pl
from jax.experimental.pallas import tpu as pltpu
from jax.sharding import PartitionSpec as P


F32, BF16 = jnp.float32, jnp.bfloat16
LOG2E = math.log2(math.e)
SUBLANES = 8
VMEM = pl.BlockSpec(memory_space=pltpu.VMEM)
SMEM = pl.BlockSpec(memory_space=pltpu.SMEM)
PARAMS = pltpu.CompilerParams(vmem_limit_bytes=8 * 2**20)


def split3(value):
    high = value.astype(BF16).astype(F32)
    rest = value - high
    middle = rest.astype(BF16).astype(F32)
    return high, middle, rest - middle


def norm_rows(value, norms_first):
    norm = jnp.sum(value * value, axis=0, keepdims=True)
    row = lax.broadcasted_iota(jnp.int32, (SUBLANES, value.shape[1]), 0)
    start = 0 if norms_first else 3
    rows = jnp.where(row < 6, 1.0, 0.0)
    for offset, addend in enumerate(split3(norm)):
        rows = jnp.where(row == start + offset, addend, rows)
    return rows


def stack(pieces):
    pieces = list(pieces)
    if sum(p.shape[0] for p in pieces) % (2 * SUBLANES):
        pieces.append(jnp.zeros_like(pieces[-1]))
    return jnp.concatenate(pieces, axis=0).astype(BF16)


def other_side(value):
    high, middle, low = split3(value)
    return stack([high, high, middle, middle, high, low, norm_rows(value, True)])


def own_side(value):
    high, middle, low = (-2.0 * part for part in split3(value))
    return stack([high, middle, high, middle, low, high, norm_rows(value, False)])


def three_kernel(scaled_dist2):
    scaled_dist2 = jnp.maximum(scaled_dist2, 1e-30)
    dist = scaled_dist2 * lax.rsqrt(scaled_dist2)
    shifted = dist + 1.5
    return (shifted * shifted + 0.75) * jnp.exp2(dist * -LOG2E)


def block_sum(dim, block, scale, own):
    points, vectors = block[:dim] * scale, block[dim:]
    dist2 = lax.dot_general(
        other_side(points), own, (((0,), (0,)), ((), ())), preferred_element_type=F32
    )
    tile = three_kernel(dist2)
    tile_high = tile.astype(BF16)
    tile_low = (tile - tile_high.astype(F32)).astype(BF16)
    vec_high = vectors.astype(BF16)
    vec = jnp.concatenate([vec_high, (vectors - vec_high.astype(F32)).astype(BF16)], axis=0)
    both = jnp.dot(vec, tile_high, preferred_element_type=F32) + jnp.dot(
        vec, tile_low, preferred_element_type=F32
    )
    return both[: vectors.shape[0]] + both[vectors.shape[0] :]


def prepare(dim, own_ref, inv_ref, noise_ref, scale_ref, side_ref, base_ref):
    row = lax.broadcasted_iota(jnp.int32, (dim, own_ref.shape[1]), 0)
    inv = jnp.zeros(row.shape, F32)
    for d in range(dim):
        inv = jnp.where(row == d, inv_ref[d], inv)
    scale = inv * math.sqrt(5.0)
    scale_ref[...] = scale
    side_ref[...] = own_side(own_ref[:dim] * scale)
    base_ref[...] = own_ref[dim:] * noise_ref[0]


def add_blocks(dim, rows, factor, blocks_ref, scale_ref, side_ref, acc_ref, *rest):
    base_ref, out_ref = rest if len(rest) == 2 else (None, rest[0])
    count = blocks_ref.shape[0] // rows
    group = math.gcd(count, 4)
    scale, own = scale_ref[...], side_ref[...]

    def step(index, total):
        for k in range(group):
            start = pl.multiple_of((index * group + k) * rows, rows)
            total = total + block_sum(dim, blocks_ref[pl.ds(start, rows)], scale, own)
        return total

    if count == group:
        total = step(0, acc_ref[...])
    else:
        total = lax.fori_loop(0, count // group, step, acc_ref[...])
    out_ref[...] = total if base_ref is None else base_ref[...] + total * factor


def cost(rows, blocks, width):
    tile = blocks // rows * width * width
    return pl.CostEstimate(flops=tile * 400, bytes_accessed=4 * blocks * width, transcendentals=2 * tile)


def on_device(points, vectors, inv_length, noise):
    count = lax.axis_size("blk")
    dim, width = points.shape
    rhs = vectors.shape[0]
    rows = dim + rhs
    small = jax.ShapeDtypeStruct((rhs, width), F32)
    own = jnp.concatenate([points, vectors], axis=0)

    def swap(value, mask):
        return lax.ppermute(value, "blk", [(i, i ^ mask) for i in range(count)])

    levels = count.bit_length() - 1
    if count != 1 << levels or levels < 2:
        pieces = [lax.all_gather(own, "blk", axis=0, tiled=True)]
    else:
        held = own
        for bit in range(levels - 1, 1, -1):
            held = jnp.concatenate([held, swap(held, 1 << bit | 1)], axis=0)
        far = swap(held, 3)
        pieces = [held, swap(held, 1), far, swap(far, 1)]

    side_rows = -(-(6 * dim + SUBLANES) // (2 * SUBLANES)) * 2 * SUBLANES
    prepare_call = pl.pallas_call(
        functools.partial(prepare, dim),
        out_shape=[
            jax.ShapeDtypeStruct((dim, width), F32),
            jax.ShapeDtypeStruct((side_rows, width), BF16),
            small,
        ],
        in_specs=[VMEM, SMEM, SMEM],
        out_specs=[VMEM] * 3,
        name="prepare",
        compiler_params=PARAMS,
        cost_estimate=pl.CostEstimate(flops=100000, bytes_accessed=4 * rows * width, transcendentals=0),
    )
    scale, side, base = prepare_call(own, inv_length, noise)

    factor = 1.0 / (3.0 * math.sqrt(width * count))
    total = jnp.zeros((rhs, width), F32)
    for index, piece in enumerate(pieces):
        last = index == len(pieces) - 1
        add_call = pl.pallas_call(
            functools.partial(add_blocks, dim, rows, factor),
            out_shape=small,
            in_specs=[VMEM] * (5 if last else 4),
            out_specs=VMEM,
            compiler_params=PARAMS,
            cost_estimate=cost(rows, piece.shape[0], width),
        )
        total = add_call(piece, scale, side, total, *([base] if last else []))
    return total


def solution(mesh):
    return jax.shard_map(
        on_device,
        mesh=mesh,
        in_specs=(P(None, ("gp", "blk")), P(None, ("gp", "blk")), P("gp"), P("gp")),
        out_specs=P(None, ("gp", "blk")),
        check_vma=False,
    )
```

time: 54.1 us -> 18.8 us (0.35)
  blocking collectives: 41.6 us -> 0 us
  matrix products: 9.97 us -> 0 us
  starting transfers between devices: 0 us -> 7.87 us
  waiting for transfers between devices: 0 us -> 4.84 us
  Pallas kernels: 0 us -> 4.41 us
  other arithmetic: 1.55 us -> 0.01 us
  local copies, waits for them, and re-layouts: 0.01 us -> 0.73 us
    all_gather x2 -> x0, blocking collectives: 41.6 us -> none  [the longest x1 23.8 us: on_device(): lax.all_gather(points, 'blk', axis=1, tiled=True)]
    dot_general x2 -> x0, matrix products: 9.97 us -> none  [the longest x1 6.41 us: matern(): jnp.dot(scaled_left.T, scaled_right, precision=lax.Precision.HIGHEST, pre...]
    ppermute x0 -> x5, starting transfers between devices: none -> 7.87 us  [swap(): return lax.ppermute(value, 'blk', [(i, i ^ mask) for i in range(count)])]
    ppermute x0 -> x5, waiting for transfers between devices: none -> 4.84 us  [swap(): return lax.ppermute(value, 'blk', [(i, i ^ mask) for i in range(count)])]
    pallas_call x0 -> x5, Pallas kernels: none -> 4.41 us  [the longest x4 3.84 us: on_device(): total = add_call(piece, scale, side, total, *([base] if last else []))]
    reduce_sum x2 -> x0, other arithmetic: 1.55 us -> none  [the longest x1 0.78 us: matern(): sq_right = jnp.sum(scaled_right * scaled_right, axis=0)]
    unnamed x2 -> x8, local copies, waits for them, and re-layouts: 0.01 us -> 0.72 us
  transfers between devices with their start and end apart: 0 -> 5, of which waited for: 0 -> 3; matrix products, arithmetic and copies ran while one was open for 0% -> 0% of each run, Pallas kernels for 0% -> 16%
where the time goes in v1:
time: 18.8 us; the launch traced here: 18.5 us
  starting transfers between devices  7.87 us (42%)
  waiting for transfers between devices  4.84 us (26%)
  Pallas kernels  4.41 us (23%)
  local copies, waits for them, and re-layouts  0.73 us (4%)
  between operations  0.69 us (4%)
    ppermute x5, starting transfers between devices, swap(): return lax.ppermute(value, 'blk', [(i, i ^ mask) for i in range(count)])  7.87 us
    ppermute x5, waiting for transfers between devices, swap(): return lax.ppermute(value, 'blk', [(i, i ^ mask) for i in range(count)])  4.84 us
    pallas_call x4, Pallas kernels, on_device(): total = add_call(piece, scale, side, total, *([base] if last else []))  3.84 us
    unnamed x8, local copies, waits for them, and re-layouts  0.72 us
    pallas_call x1, Pallas kernels, on_device(): scale, side, base = prepare_call(own, inv_length, noise)  0.57 us
  transfers between devices with their start and end apart: 5, of which 3 were waited for; matrix products, arithmetic and copies ran while one was open for 0% of the time, Pallas kernels for 16%

profile of v1, /device:TPU:0, one launch (start us, length us, event | category | flops | bytes accessed | tf_op | source)
XLA Modules:
  0.0 18.5 jit_solution(6453655811302033229)
XLA Ops:
  0.0 0.0 copy-start.2
  0.0 0.7 %constant_dynamic-update-slice_fusion.1 = (f32[16,256]{1,0:T(8,128)S(1)}, f32[64,256]{1,0:T(8,128)S(1)}) fusion(f32[8,256]{1,0:T(8,128)} %param.4), kind=kLoop, calls=%fused_computation.2 | loop fusion | bytes 24576
  0.7 0.0 copy-done.2
  0.7 0.0 copy-start.1
  0.7 3.6 %collective-permute-start = (f32[16,256]{1,0:T(8,128)S(1)}, f32[16,256]{1,0:T(8,128)S(1)}, u32[]{:S(2)}, u32[]{:S(2)}) collective-permute-start(f32[16,256]{1,0:T(8,128)S(1)} %get-tuple-element.11.own_ref), channel_id=1, source_target_pairs={{0,9},{1,8},{2,11},{3,10},{4,13},{5,12},{6,15},{7,14},{8,1},{9,0},... | collective-permute-start | bytes 49160 | tf_op jit(solution)/shard_map/ppermute | solution.py:121
  4.3 1.4 %collective-permute-done = f32[16,256]{1,0:T(8,128)S(1)} collective-permute-done((f32[16,256]{1,0:T(8,128)S(1)}, f32[16,256]{1,0:T(8,128)S(1)}, u32[]{:S(2)}, u32[]{:S(2)}) %collective-permute-start) | collective-permute-done | bytes 16416 | tf_op jit(solution)/shard_map/ppermute | solution.py:121
  5.7 0.0 copy-done.1
  5.7 1.9 %collective-permute-start.1 = (f32[32,256]{1,0:T(8,128)S(1)}, f32[32,256]{1,0:T(8,128)S(1)}, u32[]{:S(2)}, u32[]{:S(2)}) collective-permute-start(f32[32,256]{1,0:T(8,128)S(1)} %pad_maximum_fusion), channel_id=1, source_target_pairs={{0,5},{1,4},{2,7},{3,6},{4,1},{5,0},{6,3},{7,2},{8,13},{9,12},{10,... | collective-permute-start | bytes 98312 | tf_op jit(solution)/shard_map/ppermute | solution.py:121
  7.6 1.6 %collective-permute-done.1 = f32[32,256]{1,0:T(8,128)S(1)} collective-permute-done((f32[32,256]{1,0:T(8,128)S(1)}, f32[32,256]{1,0:T(8,128)S(1)}, u32[]{:S(2)}, u32[]{:S(2)}) %collective-permute-start.1) | collective-permute-done | bytes 32800 | tf_op jit(solution)/shard_map/ppermute | solution.py:121
  9.2 0.0 copy-start
  9.2 1.7 %collective-permute-start.2 = (f32[64,256]{1,0:T(8,128)S(1)}, f32[64,256]{1,0:T(8,128)S(1)}, u32[]{:S(2)}, u32[]{:S(2)}) collective-permute-start(f32[64,256]{1,0:T(8,128)S(1)} %constant_dynamic-update-slice_fusion.2.blocks_ref), channel_id=1, source_target_pairs={{0,3},{1,2},{2,1},{3,0},{4,7},{5,6},{6,5},{7,4},{8,11},{9,10},{10,... | collective-permute-start | bytes 196616 | tf_op jit(solution)/shard_map/ppermute | solution.py:121
  11.0 0.4 %collective-permute-start.4 = (f32[64,256]{1,0:T(8,128)S(1)}, f32[64,256]{1,0:T(8,128)S(1)}, u32[]{:S(2)}, u32[]{:S(2)}) collective-permute-start(f32[64,256]{1,0:T(8,128)S(1)} %constant_dynamic-update-slice_fusion.2.blocks_ref), channel_id=1, source_target_pairs={{0,1},{1,0},{2,3},{3,2},{4,5},{5,4},{6,7},{7,6},{8,9},{9,8},{10,11... | collective-permute-start | bytes 196616 | tf_op jit(solution)/shard_map/ppermute | solution.py:121
  11.4 1.8 %collective-permute-done.2.blocks_ref = f32[64,256]{1,0:T(8,128)S(1)} collective-permute-done((f32[64,256]{1,0:T(8,128)S(1)}, f32[64,256]{1,0:T(8,128)S(1)}, u32[]{:S(2)}, u32[]{:S(2)}) %collective-permute-start.2) | collective-permute-done | bytes 65568 | tf_op jit(solution)/shard_map/ppermute | solution.py:121
  13.2 0.3 %collective-permute-start.3 = (f32[64,256]{1,0:T(8,128)S(1)}, f32[64,256]{1,0:T(8,128)S(1)}, u32[]{:S(2)}, u32[]{:S(2)}) collective-permute-start(f32[64,256]{1,0:T(8,128)S(1)} %collective-permute-done.2.blocks_ref), channel_id=1, source_target_pairs={{0,1},{1,0},{2,3},{3,2},{4,5},{5,4},{6,7},{7,6},{8,9},{9,8},{10,11... | collective-permute-start | bytes 196616 | tf_op jit(solution)/shard_map/ppermute | solution.py:121
  14.1 0.0 copy-done
  14.1 0.6 %prepare.1 = (f32[8,256]{1,0:T(8,128)S(1)}, bf16[64,256]{1,0:T(8,128)(2,1)S(1)}, f32[8,256]{1,0:T(8,128)S(1)}) custom-call(f32[16,256]{1,0:T(8,128)S(1)} %get-tuple-element.11.own_ref, f32[8]{0:T(128)S(1)} %copy-done, f32[1]{0:T(128)S(6)} %copy.9.noise_ref), custom_call_target="tpu_custom_call" | custom-call | flops 100000 | bytes 16384 | tf_op jit(solution)/shard_map/prepare/pallas_call | solution.py:147
  14.7 0.8 %shard_map.46.acc_ref = f32[8,256]{1,0:T(8,128)S(1)} custom-call(f32[64,256]{1,0:T(8,128)S(1)} %constant_dynamic-update-slice_fusion.2.blocks_ref, f32[8,256]{1,0:T(8,128)S(1)} %get-tuple-element.8.scale_ref, bf16[64,256]{1,0:T(8,128)(2,1)S(1)} %get-tuple-element.9.side_ref, f32[8,256]{1,0:T(8,128)S(1)} %broadcast_in_dim.3.acc_ref), custom_call_target="tpu_custom_call" | custom-call | flops 104857600 | bytes 65536 | tf_op jit(solution)/shard_map/pallas_call | solution.py:161
  15.5 0.0 collective-permute-done.4.blocks_ref
  15.5 0.8 %shard_map.47.acc_ref = f32[8,256]{1,0:T(8,128)S(1)} custom-call(f32[64,256]{1,0:T(8,128)S(1)} %collective-permute-done.4.blocks_ref, f32[8,256]{1,0:T(8,128)S(1)} %get-tuple-element.8.scale_ref, bf16[64,256]{1,0:T(8,128)(2,1)S(1)} %get-tuple-element.9.side_ref, f32[8,256]{1,0:T(8,128)S(1)} %shard_map.46.acc_ref), custom_call_target="tpu_custom_call" | custom-call | flops 104857600 | bytes 65536 | tf_op jit(solution)/shard_map/pallas_call | solution.py:161
  16.3 0.8 %shard_map.48.acc_ref = f32[8,256]{1,0:T(8,128)S(1)} custom-call(f32[64,256]{1,0:T(8,128)S(1)} %collective-permute-done.2.blocks_ref, f32[8,256]{1,0:T(8,128)S(1)} %get-tuple-element.8.scale_ref, bf16[64,256]{1,0:T(8,128)(2,1)S(1)} %get-tuple-element.9.side_ref, f32[8,256]{1,0:T(8,128)S(1)} %shard_map.47.acc_ref), custom_call_target="tpu_custom_call" | custom-call | flops 104857600 | bytes 65536 | tf_op jit(solution)/shard_map/pallas_call | solution.py:161
  17.1 0.0 collective-permute-done.3.blocks_ref
  17.1 1.4 %shard_map.49 = f32[8,256]{1,0:T(8,128)} custom-call(f32[64,256]{1,0:T(8,128)S(1)} %collective-permute-done.3.blocks_ref, f32[8,256]{1,0:T(8,128)S(1)} %get-tuple-element.8.scale_ref, bf16[64,256]{1,0:T(8,128)(2,1)S(1)} %get-tuple-element.9.side_ref, f32[8,256]{1,0:T(8,128)S(1)} %shard_map.48.acc_ref, f32[8,256]{1,0:T(8,128)S(1)} %get-tuple-element.10.rest_0_), custom_call_target="tpu_custom_call" | custom-call | flops 104857600 | bytes 65536 | tf_op jit(solution)/shard_map/pallas_call | solution.py:161
  (5 shorter events, 0.0 us)
Async XLA Ops:
  0.0 0.7 %copy-start.2 = (f32[8,256]{1,0:T(8,128)S(1)}, f32[8,256]{1,0:T(8,128)}, u32[]{:S(2)}) copy-start(f32[8,256]{1,0:T(8,128)} %param.5) | copy-start | bytes 24580
  0.7 5.0 %copy-start.1 = (f32[8,256]{1,0:T(8,128)S(1)}, f32[8,256]{1,0:T(8,128)}, u32[]{:S(2)}) copy-start(f32[8,256]{1,0:T(8,128)} %param.4) | copy-start | bytes 24580
  0.7 5.0 %collective-permute-start = (f32[16,256]{1,0:T(8,128)S(1)}, f32[16,256]{1,0:T(8,128)S(1)}, u32[]{:S(2)}, u32[]{:S(2)}) collective-permute-start(f32[16,256]{1,0:T(8,128)S(1)} %get-tuple-element.11.own_ref), channel_id=1, source_target_pairs={{0,9},{1,8},{2,11},{3,10},{4,13},{5,12},{6,15},{7,14},{8,1},{9,0},... | collective-permute-start | bytes 49160 | tf_op jit(solution)/shard_map/ppermute | solution.py:121
  5.7 3.5 %collective-permute-start.1 = (f32[32,256]{1,0:T(8,128)S(1)}, f32[32,256]{1,0:T(8,128)S(1)}, u32[]{:S(2)}, u32[]{:S(2)}) collective-permute-start(f32[32,256]{1,0:T(8,128)S(1)} %pad_maximum_fusion), channel_id=1, source_target_pairs={{0,5},{1,4},{2,7},{3,6},{4,1},{5,0},{6,3},{7,2},{8,13},{9,12},{10,... | collective-permute-start | bytes 98312 | tf_op jit(solution)/shard_map/ppermute | solution.py:121
  9.2 4.9 %copy-start = (f32[8]{0:T(128)S(1)}, f32[8]{0:T(128)}, u32[]{:S(2)}) copy-start(f32[8]{0:T(128)} %inv_ref.1) | copy-start | bytes 100
  9.2 3.9 %collective-permute-start.2 = (f32[64,256]{1,0:T(8,128)S(1)}, f32[64,256]{1,0:T(8,128)S(1)}, u32[]{:S(2)}, u32[]{:S(2)}) collective-permute-start(f32[64,256]{1,0:T(8,128)S(1)} %constant_dynamic-update-slice_fusion.2.blocks_ref), channel_id=1, source_target_pairs={{0,3},{1,2},{2,1},{3,0},{4,7},{5,6},{6,5},{7,4},{8,11},{9,10},{10,... | collective-permute-start | bytes 196616 | tf_op jit(solution)/shard_map/ppermute | solution.py:121
  11.0 4.5 %collective-permute-start.4 = (f32[64,256]{1,0:T(8,128)S(1)}, f32[64,256]{1,0:T(8,128)S(1)}, u32[]{:S(2)}, u32[]{:S(2)}) collective-permute-start(f32[64,256]{1,0:T(8,128)S(1)} %constant_dynamic-update-slice_fusion.2.blocks_ref), channel_id=1, source_target_pairs={{0,1},{1,0},{2,3},{3,2},{4,5},{5,4},{6,7},{7,6},{8,9},{9,8},{10,11... | collective-permute-start | bytes 196616 | tf_op jit(solution)/shard_map/ppermute | solution.py:121
  13.2 3.9 %collective-permute-start.3 = (f32[64,256]{1,0:T(8,128)S(1)}, f32[64,256]{1,0:T(8,128)S(1)}, u32[]{:S(2)}, u32[]{:S(2)}) collective-permute-start(f32[64,256]{1,0:T(8,128)S(1)} %collective-permute-done.2.blocks_ref), channel_id=1, source_target_pairs={{0,1},{1,0},{2,3},{3,2},{4,5},{5,4},{6,7},{7,6},{8,9},{9,8},{10,11... | collective-permute-start | bytes 196616 | tf_op jit(solution)/shard_map/ppermute | solution.py:121

commit v2 on v1

--- a/solution.py
+++ b/solution.py
@@ -85,28 +85,26 @@
     base_ref[...] = own_ref[dim:] * noise_ref[0]
 
 
-def add_blocks(dim, rows, factor, blocks_ref, scale_ref, side_ref, acc_ref, *rest):
-    base_ref, out_ref = rest if len(rest) == 2 else (None, rest[0])
-    count = blocks_ref.shape[0] // rows
-    group = math.gcd(count, 4)
+def add_pieces(dim, rows, factor, scale_ref, side_ref, acc_ref, *rest):
+    *rest, out_ref = rest
+    base_ref = rest.pop(0) if factor else None
     scale, own = scale_ref[...], side_ref[...]
+    total = acc_ref[...]
+    for piece_ref in rest:
+        count = piece_ref.shape[0] // rows
+        group = math.gcd(count, 4)
 
-    def step(index, total):
-        for k in range(group):
-            start = pl.multiple_of((index * group + k) * rows, rows)
-            total = total + block_sum(dim, blocks_ref[pl.ds(start, rows)], scale, own)
-        return total
+        def step(index, total, piece_ref=piece_ref, group=group):
+            for k in range(group):
+                start = pl.multiple_of((index * group + k) * rows, rows)
+                total = total + block_sum(dim, piece_ref[pl.ds(start, rows)], scale, own)
+            return total
 
-    if count == group:
-        total = step(0, acc_ref[...])
-    else:
-        total = lax.fori_loop(0, count // group, step, acc_ref[...])
-    out_ref[...] = total if base_ref is None else base_ref[...] + total * factor
-
-
-def cost(rows, blocks, width):
-    tile = blocks // rows * width * width
-    return pl.CostEstimate(flops=tile * 400, bytes_accessed=4 * blocks * width, transcendentals=2 * tile)
+        if count == group:
+            total = step(0, total)
+        else:
+            total = lax.fori_loop(0, count // group, step, total)
+    out_ref[...] = base_ref[...] + total * factor if factor else total
 
 
 def on_device(points, vectors, inv_length, noise):
@@ -121,14 +119,19 @@
         return lax.ppermute(value, "blk", [(i, i ^ mask) for i in range(count)])
 
     levels = count.bit_length() - 1
-    if count != 1 << levels or levels < 2:
-        pieces = [lax.all_gather(own, "blk", axis=0, tiled=True)]
+    if count != 1 << levels or levels < 3:
+        groups = [[lax.all_gather(own, "blk", axis=0, tiled=True)]]
     else:
         held = own
-        for bit in range(levels - 1, 1, -1):
+        for bit in range(levels - 1, 2, -1):
             held = jnp.concatenate([held, swap(held, 1 << bit | 1)], axis=0)
-        far = swap(held, 3)
-        pieces = [held, swap(held, 1), far, swap(far, 1)]
+        newest = swap(held, 5)
+        early = swap(held, 3)
+        late = swap(newest, 3)
+        near = swap(jnp.concatenate([held, newest], axis=0), 1)
+        early_core = swap(early, 1)
+        late_core = swap(late, 1)
+        groups = [[held, newest], [near], [early, early_core, late], [late_core]]
 
     side_rows = -(-(6 * dim + SUBLANES) // (2 * SUBLANES)) * 2 * SUBLANES
     prepare_call = pl.pallas_call(
@@ -148,17 +151,23 @@
 
     factor = 1.0 / (3.0 * math.sqrt(width * count))
     total = jnp.zeros((rhs, width), F32)
-    for index, piece in enumerate(pieces):
-        last = index == len(pieces) - 1
+    for index, pieces in enumerate(groups):
+        last = index == len(groups) - 1
+        operands = [scale, side, total] + ([base] if last else []) + pieces
+        blocks = sum(piece.shape[0] for piece in pieces) // rows
         add_call = pl.pallas_call(
-            functools.partial(add_blocks, dim, rows, factor),
+            functools.partial(add_pieces, dim, rows, factor if last else None),
             out_shape=small,
-            in_specs=[VMEM] * (5 if last else 4),
+            in_specs=[VMEM] * len(operands),
             out_specs=VMEM,
             compiler_params=PARAMS,
-            cost_estimate=cost(rows, piece.shape[0], width),
+            cost_estimate=pl.CostEstimate(
+                flops=blocks * width * width * 400,
+                bytes_accessed=4 * blocks * rows * width,
+                transcendentals=2 * blocks * width * width,
+            ),
         )
-        total = add_call(piece, scale, side, total, *([base] if last else []))
+        total = add_call(*operands)
     return total
 
 

time: 18.8 us -> 19.2 us (1.021)
    ppermute x5 -> x7, starting transfers between devices: 7.87 us -> 8.06 us  [swap(): return lax.ppermute(value, 'blk', [(i, i ^ mask) for i in range(count)])]
    ppermute x5 -> x7, waiting for transfers between devices: 4.84 us -> 4.97 us  [swap(): return lax.ppermute(value, 'blk', [(i, i ^ mask) for i in range(count)])]
  transfers between devices with their start and end apart: 5 -> 7, of which waited for: 3 -> 4; matrix products, arithmetic and copies ran while one was open for 0% -> 0% of each run, Pallas kernels for 16% -> 17%
where the time goes in v2:
time: 19.2 us; the launch traced here: 18.9 us
  starting transfers between devices  8.06 us (42%)
  waiting for transfers between devices  4.97 us (26%)
  Pallas kernels  4.44 us (23%)
  local copies, waits for them, and re-layouts  0.73 us (4%)
  between operations  0.69 us (4%)
    ppermute x7, starting transfers between devices, swap(): return lax.ppermute(value, 'blk', [(i, i ^ mask) for i in range(count)])  8.06 us
    ppermute x7, waiting for transfers between devices, swap(): return lax.ppermute(value, 'blk', [(i, i ^ mask) for i in range(count)])  4.97 us
    pallas_call x4, Pallas kernels, on_device(): total = add_call(*operands)  3.87 us
    unnamed x8, local copies, waits for them, and re-layouts  0.73 us
    pallas_call x1, Pallas kernels, on_device(): scale, side, base = prepare_call(own, inv_length, noise)  0.57 us
  transfers between devices with their start and end apart: 7, of which 4 were waited for; matrix products, arithmetic and copies ran while one was open for 0% of the time, Pallas kernels for 17%

profile of v2, /device:TPU:0, one launch (start us, length us, event | category | flops | bytes accessed | tf_op | source)
XLA Modules:
  0.0 18.9 jit_solution(4940928812131833926)
XLA Ops:
  0.0 0.0 copy-start.2
  0.0 0.7 %constant_dynamic-update-slice_fusion.4 = (f32[32,256]{1,0:T(8,128)S(1)}, f32[16,256]{1,0:T(8,128)S(1)}) fusion(f32[8,256]{1,0:T(8,128)} %param.4), kind=kLoop, calls=%fused_computation.5 | loop fusion | bytes 24576
  0.7 0.0 copy-done.2
  0.7 3.5 %collective-permute-start = (f32[16,256]{1,0:T(8,128)S(1)}, f32[16,256]{1,0:T(8,128)S(1)}, u32[]{:S(2)}, u32[]{:S(2)}) collective-permute-start(f32[16,256]{1,0:T(8,128)S(1)} %get-tuple-element.12.own_ref), channel_id=1, source_target_pairs={{0,9},{1,8},{2,11},{3,10},{4,13},{5,12},{6,15},{7,14},{8,1},{9,0},... | collective-permute-start | bytes 49160 | tf_op jit(solution)/shard_map/ppermute | solution.py:119
  4.2 1.4 %collective-permute-done = f32[16,256]{1,0:T(8,128)S(1)} collective-permute-done((f32[16,256]{1,0:T(8,128)S(1)}, f32[16,256]{1,0:T(8,128)S(1)}, u32[]{:S(2)}, u32[]{:S(2)}) %collective-permute-start) | collective-permute-done | bytes 16416 | tf_op jit(solution)/shard_map/ppermute | solution.py:119
  5.7 0.0 copy-start.1
  5.7 1.9 %collective-permute-start.1 = (f32[32,256]{1,0:T(8,128)S(1)}, f32[32,256]{1,0:T(8,128)S(1)}, u32[]{:S(2)}, u32[]{:S(2)}) collective-permute-start(f32[32,256]{1,0:T(8,128)S(1)} %constant_dynamic-update-slice_fusion.2.rest_0_), channel_id=1, source_target_pairs={{0,5},{1,4},{2,7},{3,6},{4,1},{5,0},{6,3},{7,2},{8,13},{9,12},{10,... | collective-permute-start | bytes 98312 | tf_op jit(solution)/shard_map/ppermute | solution.py:119
  7.6 1.6 %collective-permute-done.1.rest_1_ = f32[32,256]{1,0:T(8,128)S(1)} collective-permute-done((f32[32,256]{1,0:T(8,128)S(1)}, f32[32,256]{1,0:T(8,128)S(1)}, u32[]{:S(2)}, u32[]{:S(2)}) %collective-permute-start.1) | collective-permute-done | bytes 32800 | tf_op jit(solution)/shard_map/ppermute | solution.py:119
  9.2 0.0 copy-done.1
  9.2 0.0 copy-start
  9.2 0.6 %collective-permute-start.2 = (f32[64,256]{1,0:T(8,128)S(1)}, f32[64,256]{1,0:T(8,128)S(1)}, u32[]{:S(2)}, u32[]{:S(2)}) collective-permute-start(f32[64,256]{1,0:T(8,128)S(1)} %pad_maximum_fusion), channel_id=1, source_target_pairs={{0,1},{1,0},{2,3},{3,2},{4,5},{5,4},{6,7},{7,6},{8,9},{9,8},{10,11... | collective-permute-start | bytes 196616 | tf_op jit(solution)/shard_map/ppermute | solution.py:119
  9.8 1.6 %collective-permute-start.3 = (f32[32,256]{1,0:T(8,128)S(1)}, f32[32,256]{1,0:T(8,128)S(1)}, u32[]{:S(2)}, u32[]{:S(2)}) collective-permute-start(f32[32,256]{1,0:T(8,128)S(1)} %constant_dynamic-update-slice_fusion.2.rest_0_), channel_id=1, source_target_pairs={{0,3},{1,2},{2,1},{3,0},{4,7},{5,6},{6,5},{7,4},{8,11},{9,10},{10,... | collective-permute-start | bytes 98312 | tf_op jit(solution)/shard_map/ppermute | solution.py:119
  11.4 0.1 collective-permute-start.5
  11.5 1.7 %collective-permute-done.3.rest_0_ = f32[32,256]{1,0:T(8,128)S(1)} collective-permute-done((f32[32,256]{1,0:T(8,128)S(1)}, f32[32,256]{1,0:T(8,128)S(1)}, u32[]{:S(2)}, u32[]{:S(2)}) %collective-permute-start.3) | collective-permute-done | bytes 32800 | tf_op jit(solution)/shard_map/ppermute | solution.py:119
  13.2 0.1 collective-permute-start.4
  14.0 0.0 copy-done
  14.0 0.6 %prepare.1 = (f32[8,256]{1,0:T(8,128)S(1)}, bf16[64,256]{1,0:T(8,128)(2,1)S(1)}, f32[8,256]{1,0:T(8,128)S(1)}) custom-call(f32[16,256]{1,0:T(8,128)S(1)} %get-tuple-element.12.own_ref, f32[8]{0:T(128)S(1)} %copy-done, f32[1]{0:T(128)S(6)} %copy.8.noise_ref), custom_call_target="tpu_custom_call" | custom-call | flops 100000 | bytes 16384 | tf_op jit(solution)/shard_map/prepare/pallas_call | solution.py:150
  14.5 0.2 %collective-permute-done.5.rest_2_ = f32[32,256]{1,0:T(8,128)S(1)} collective-permute-done((f32[32,256]{1,0:T(8,128)S(1)}, f32[32,256]{1,0:T(8,128)S(1)}, u32[]{:S(2)}, u32[]{:S(2)}) %collective-permute-start.5) | collective-permute-done | bytes 32800 | tf_op jit(solution)/shard_map/ppermute | solution.py:119
  14.8 0.2 %collective-permute-start.6 = (f32[32,256]{1,0:T(8,128)S(1)}, f32[32,256]{1,0:T(8,128)S(1)}, u32[]{:S(2)}, u32[]{:S(2)}) collective-permute-start(f32[32,256]{1,0:T(8,128)S(1)} %collective-permute-done.5.rest_2_), channel_id=1, source_target_pairs={{0,1},{1,0},{2,3},{3,2},{4,5},{5,4},{6,7},{7,6},{8,9},{9,8},{10,11... | collective-permute-start | bytes 98312 | tf_op jit(solution)/shard_map/ppermute | solution.py:119
  15.0 0.8 %shard_map.46.acc_ref = f32[8,256]{1,0:T(8,128)S(1)} custom-call(f32[8,256]{1,0:T(8,128)S(1)} %get-tuple-element.8.scale_ref, bf16[64,256]{1,0:T(8,128)(2,1)S(1)} %get-tuple-element.9.side_ref, f32[8,256]{1,0:T(8,128)S(1)} %broadcast_in_dim.3.acc_ref, f32[32,256]{1,0:T(8,128)S(1)} %constant_dynamic-update-slice_fusion.2.rest_0_, ...), custom_call_target="tpu_custom_call" | custom-call | flops 104857600 | bytes 65536 | tf_op jit(solution)/shard_map/pallas_call | solution.py:170
  15.8 0.0 collective-permute-done.2.rest_0_
  15.8 0.8 %shard_map.47.acc_ref = f32[8,256]{1,0:T(8,128)S(1)} custom-call(f32[8,256]{1,0:T(8,128)S(1)} %get-tuple-element.8.scale_ref, bf16[64,256]{1,0:T(8,128)(2,1)S(1)} %get-tuple-element.9.side_ref, f32[8,256]{1,0:T(8,128)S(1)} %shard_map.46.acc_ref, f32[64,256]{1,0:T(8,128)S(1)} %collective-permute-done.2.rest_0_), custom_call_target="tpu_custom_call" | custom-call | flops 104857600 | bytes 65536 | tf_op jit(solution)/shard_map/pallas_call | solution.py:170
  16.6 0.0 collective-permute-done.4.rest_1_
  16.6 1.1 %shard_map.48.acc_ref = f32[8,256]{1,0:T(8,128)S(1)} custom-call(f32[8,256]{1,0:T(8,128)S(1)} %get-tuple-element.8.scale_ref, bf16[64,256]{1,0:T(8,128)(2,1)S(1)} %get-tuple-element.9.side_ref, f32[8,256]{1,0:T(8,128)S(1)} %shard_map.47.acc_ref, f32[32,256]{1,0:T(8,128)S(1)} %collective-permute-done.3.rest_0_, f32[32,256]{1,0:T(8,128)S(1)} %collective-permute-done.4.rest_1_, ...), custom_call_target="tpu_custom_call" | custom-call | flops 157286400 | bytes 98304 | tf_op jit(solution)/shard_map/pallas_call | solution.py:170
  17.7 0.0 collective-permute-done.6.rest_1_
  17.7 1.2 %shard_map.49 = f32[8,256]{1,0:T(8,128)} custom-call(f32[8,256]{1,0:T(8,128)S(1)} %get-tuple-element.8.scale_ref, bf16[64,256]{1,0:T(8,128)(2,1)S(1)} %get-tuple-element.9.side_ref, f32[8,256]{1,0:T(8,128)S(1)} %shard_map.48.acc_ref, f32[8,256]{1,0:T(8,128)S(1)} %get-tuple-element.10.rest_0_, f32[32,256]{1,0:T(8,128)S(1)} %collective-permute-done.6.rest_1_), custom_call_target="tpu_custom_call" | custom-call | flops 52428800 | bytes 32768 | tf_op jit(solution)/shard_map/pallas_call | solution.py:170
  (4 shorter events, 0.0 us)
Async XLA Ops:
  0.0 0.7 %copy-start.2 = (f32[8,256]{1,0:T(8,128)S(1)}, f32[8,256]{1,0:T(8,128)}, u32[]{:S(2)}) copy-start(f32[8,256]{1,0:T(8,128)} %param.5) | copy-start | bytes 24580
  0.7 4.9 %collective-permute-start = (f32[16,256]{1,0:T(8,128)S(1)}, f32[16,256]{1,0:T(8,128)S(1)}, u32[]{:S(2)}, u32[]{:S(2)}) collective-permute-start(f32[16,256]{1,0:T(8,128)S(1)} %get-tuple-element.12.own_ref), channel_id=1, source_target_pairs={{0,9},{1,8},{2,11},{3,10},{4,13},{5,12},{6,15},{7,14},{8,1},{9,0},... | collective-permute-start | bytes 49160 | tf_op jit(solution)/shard_map/ppermute | solution.py:119
  5.7 3.5 %copy-start.1 = (f32[8,256]{1,0:T(8,128)S(1)}, f32[8,256]{1,0:T(8,128)}, u32[]{:S(2)}) copy-start(f32[8,256]{1,0:T(8,128)} %param.4) | copy-start | bytes 24580
  5.7 3.5 %collective-permute-start.1 = (f32[32,256]{1,0:T(8,128)S(1)}, f32[32,256]{1,0:T(8,128)S(1)}, u32[]{:S(2)}, u32[]{:S(2)}) collective-permute-start(f32[32,256]{1,0:T(8,128)S(1)} %constant_dynamic-update-slice_fusion.2.rest_0_), channel_id=1, source_target_pairs={{0,5},{1,4},{2,7},{3,6},{4,1},{5,0},{6,3},{7,2},{8,13},{9,12},{10,... | collective-permute-start | bytes 98312 | tf_op jit(solution)/shard_map/ppermute | solution.py:119
  9.2 4.8 %copy-start = (f32[8]{0:T(128)S(1)}, f32[8]{0:T(128)}, u32[]{:S(2)}) copy-start(f32[8]{0:T(128)} %inv_ref.1) | copy-start | bytes 100
  9.2 6.6 %collective-permute-start.2 = (f32[64,256]{1,0:T(8,128)S(1)}, f32[64,256]{1,0:T(8,128)S(1)}, u32[]{:S(2)}, u32[]{:S(2)}) collective-permute-start(f32[64,256]{1,0:T(8,128)S(1)} %pad_maximum_fusion), channel_id=1, source_target_pairs={{0,1},{1,0},{2,3},{3,2},{4,5},{5,4},{6,7},{7,6},{8,9},{9,8},{10,11... | collective-permute-start | bytes 196616 | tf_op jit(solution)/shard_map/ppermute | solution.py:119
  9.8 3.4 %collective-permute-start.3 = (f32[32,256]{1,0:T(8,128)S(1)}, f32[32,256]{1,0:T(8,128)S(1)}, u32[]{:S(2)}, u32[]{:S(2)}) collective-permute-start(f32[32,256]{1,0:T(8,128)S(1)} %constant_dynamic-update-slice_fusion.2.rest_0_), channel_id=1, source_target_pairs={{0,3},{1,2},{2,1},{3,0},{4,7},{5,6},{6,5},{7,4},{8,11},{9,10},{10,... | collective-permute-start | bytes 98312 | tf_op jit(solution)/shard_map/ppermute | solution.py:119
  11.4 3.4 %collective-permute-start.5 = (f32[32,256]{1,0:T(8,128)S(1)}, f32[32,256]{1,0:T(8,128)S(1)}, u32[]{:S(2)}, u32[]{:S(2)}) collective-permute-start(f32[32,256]{1,0:T(8,128)S(1)} %collective-permute-done.1.rest_1_), channel_id=1, source_target_pairs={{0,3},{1,2},{2,1},{3,0},{4,7},{5,6},{6,5},{7,4},{8,11},{9,10},{10,... | collective-permute-start | bytes 98312 | tf_op jit(solution)/shard_map/ppermute | solution.py:119
  13.2 3.4 %collective-permute-start.4 = (f32[32,256]{1,0:T(8,128)S(1)}, f32[32,256]{1,0:T(8,128)S(1)}, u32[]{:S(2)}, u32[]{:S(2)}) collective-permute-start(f32[32,256]{1,0:T(8,128)S(1)} %collective-permute-done.3.rest_0_), channel_id=1, source_target_pairs={{0,1},{1,0},{2,3},{3,2},{4,5},{5,4},{6,7},{7,6},{8,9},{9,8},{10,11... | collective-permute-start | bytes 98312 | tf_op jit(solution)/shard_map/ppermute | solution.py:119
  14.8 2.9 %collective-permute-start.6 = (f32[32,256]{1,0:T(8,128)S(1)}, f32[32,256]{1,0:T(8,128)S(1)}, u32[]{:S(2)}, u32[]{:S(2)}) collective-permute-start(f32[32,256]{1,0:T(8,128)S(1)} %collective-permute-done.5.rest_2_), channel_id=1, source_target_pairs={{0,1},{1,0},{2,3},{3,2},{4,5},{5,4},{6,7},{7,6},{8,9},{9,8},{10,11... | collective-permute-start | bytes 98312 | tf_op jit(solution)/shard_map/ppermute | solution.py:119

commit v3 on v2

--- a/solution.py
+++ b/solution.py
@@ -13,7 +13,6 @@
 LOG2E = math.log2(math.e)
 SUBLANES = 8
 VMEM = pl.BlockSpec(memory_space=pltpu.VMEM)
-SMEM = pl.BlockSpec(memory_space=pltpu.SMEM)
 PARAMS = pltpu.CompilerParams(vmem_limit_bytes=8 * 2**20)
 
 
@@ -51,38 +50,48 @@
     return stack([high, middle, high, middle, low, high, norm_rows(value, False)])
 
 
-def three_kernel(scaled_dist2):
-    scaled_dist2 = jnp.maximum(scaled_dist2, 1e-30)
-    dist = scaled_dist2 * lax.rsqrt(scaled_dist2)
-    shifted = dist + 1.5
-    return (shifted * shifted + 0.75) * jnp.exp2(dist * -LOG2E)
+def third_kernel(value):
+    value = jnp.maximum(value, 1e-30)
+    third = value * lax.rsqrt(value)
+    return (value + third + 1.0 / 3.0) * jnp.exp2(third * (-3.0 * LOG2E))
 
 
 def block_sum(dim, block, scale, own):
     points, vectors = block[:dim] * scale, block[dim:]
-    dist2 = lax.dot_general(
-        other_side(points), own, (((0,), (0,)), ((), ())), preferred_element_type=F32
-    )
-    tile = three_kernel(dist2)
-    tile_high = tile.astype(BF16)
-    tile_low = (tile - tile_high.astype(F32)).astype(BF16)
+    width = block.shape[1]
+    other = other_side(points)
     vec_high = vectors.astype(BF16)
     vec = jnp.concatenate([vec_high, (vectors - vec_high.astype(F32)).astype(BF16)], axis=0)
-    both = jnp.dot(vec, tile_high, preferred_element_type=F32) + jnp.dot(
-        vec, tile_low, preferred_element_type=F32
-    )
+    part = width // 2 if width % 256 == 0 else width
+    both = 0.0
+    for start in range(0, width, part):
+        here = slice(start, start + part)
+        value = lax.dot_general(
+            other[:, here], own, (((0,), (0,)), ((), ())), preferred_element_type=F32
+        )
+        tile = third_kernel(value)
+        high = tile.astype(BF16)
+        low = (tile - high.astype(F32)).astype(BF16)
+        both += jnp.dot(
+            jnp.concatenate([vec[:, here]] * 2, axis=1),
+            jnp.concatenate([high, low], axis=0),
+            preferred_element_type=F32,
+        )
     return both[: vectors.shape[0]] + both[vectors.shape[0] :]
 
 
-def prepare(dim, own_ref, inv_ref, noise_ref, scale_ref, side_ref, base_ref):
-    row = lax.broadcasted_iota(jnp.int32, (dim, own_ref.shape[1]), 0)
-    inv = jnp.zeros(row.shape, F32)
-    for d in range(dim):
-        inv = jnp.where(row == d, inv_ref[d], inv)
-    scale = inv * math.sqrt(5.0)
+def prepare(dim, own_ref, params_ref, scale_ref, side_ref, base_ref, sum_ref):
+    here = lax.broadcasted_iota(jnp.int32, (dim, dim), 0) == lax.broadcasted_iota(
+        jnp.int32, (dim, dim), 1
+    )
+    params = params_ref[...].reshape(1, dim + 1)
+    inv = jnp.sum(jnp.where(here, params[:, :dim], 0.0), axis=1, keepdims=True)
+    scale = jnp.broadcast_to(inv * (math.sqrt(5.0) / 3.0), scale_ref.shape)
+    side = own_side(own_ref[:dim] * scale)
     scale_ref[...] = scale
-    side_ref[...] = own_side(own_ref[:dim] * scale)
-    base_ref[...] = own_ref[dim:] * noise_ref[0]
+    side_ref[...] = side
+    base_ref[...] = own_ref[dim:] * params[:, dim:]
+    sum_ref[...] = block_sum(dim, own_ref[...], scale, side)
 
 
 def add_pieces(dim, rows, factor, scale_ref, side_ref, acc_ref, *rest):
@@ -113,25 +122,28 @@
     rhs = vectors.shape[0]
     rows = dim + rhs
     small = jax.ShapeDtypeStruct((rhs, width), F32)
-    own = jnp.concatenate([points, vectors], axis=0)
+    own = lax.optimization_barrier(jnp.concatenate([points, vectors], axis=0))
+    params = lax.optimization_barrier(jnp.concatenate([inv_length, noise]))
 
     def swap(value, mask):
         return lax.ppermute(value, "blk", [(i, i ^ mask) for i in range(count)])
 
     levels = count.bit_length() - 1
     if count != 1 << levels or levels < 3:
-        groups = [[lax.all_gather(own, "blk", axis=0, tiled=True)]]
+        others = [lax.ppermute(own, "blk", [(i, (i + k) % count) for i in range(count)]) for k in range(1, count)]
+        groups = [others + [newest, early], [early_core, near, late], [late_core]]
     else:
-        held = own
+        held, others = own, []
         for bit in range(levels - 1, 2, -1):
-            held = jnp.concatenate([held, swap(held, 1 << bit | 1)], axis=0)
+            others.append(swap(held, 1 << bit | 1))
+            held = jnp.concatenate([held, others[-1]], axis=0)
         newest = swap(held, 5)
         early = swap(held, 3)
         late = swap(newest, 3)
         near = swap(jnp.concatenate([held, newest], axis=0), 1)
         early_core = swap(early, 1)
         late_core = swap(late, 1)
-        groups = [[held, newest], [near], [early, early_core, late], [late_core]]
+        groups = [others + [newest, early], [early_core, near, late], [late_core]]
 
     side_rows = -(-(6 * dim + SUBLANES) // (2 * SUBLANES)) * 2 * SUBLANES
     prepare_call = pl.pallas_call(
@@ -140,17 +152,17 @@
             jax.ShapeDtypeStruct((dim, width), F32),
             jax.ShapeDtypeStruct((side_rows, width), BF16),
             small,
+            small,
         ],
-        in_specs=[VMEM, SMEM, SMEM],
-        out_specs=[VMEM] * 3,
+        in_specs=[VMEM] * 2,
+        out_specs=[VMEM] * 4,
         name="prepare",
         compiler_params=PARAMS,
         cost_estimate=pl.CostEstimate(flops=100000, bytes_accessed=4 * rows * width, transcendentals=0),
     )
-    scale, side, base = prepare_call(own, inv_length, noise)
+    scale, side, base, total = prepare_call(own, params)
 
-    factor = 1.0 / (3.0 * math.sqrt(width * count))
-    total = jnp.zeros((rhs, width), F32)
+    factor = 3.0 / math.sqrt(width * count)
     for index, pieces in enumerate(groups):
         last = index == len(groups) - 1
         operands = [scale, side, total] + ([base] if last else []) + pieces

time: 19.2 us -> 17.3 us (0.901)
  waiting for transfers between devices: 4.97 us -> 2.97 us
  starting transfers between devices: 8.06 us -> 8.97 us
  Pallas kernels: 4.44 us -> 3.61 us
  other arithmetic: 0.01 us -> 0.8 us
  local copies, waits for them, and re-layouts: 0.73 us -> 0.01 us
    ppermute x7, waiting for transfers between devices: 4.97 us -> 2.97 us  [swap(): return lax.ppermute(value, 'blk', [(i, i ^ mask) for i in range(count)])]
    ppermute x7, starting transfers between devices: 8.06 us -> 8.97 us  [swap(): return lax.ppermute(value, 'blk', [(i, i ^ mask) for i in range(count)])]
    concatenate x0 -> x3, other arithmetic: none -> 0.79 us  [the longest x1 0.72 us: on_device(): own = lax.optimization_barrier(jnp.concatenate([points, vectors], axis=0))]
    pallas_call x4 -> x3, Pallas kernels: 3.87 us -> 3.12 us  [on_device(): total = add_call(*operands)]
    unnamed x8 -> x2, local copies, waits for them, and re-layouts: 0.73 us -> 0.01 us
  transfers between devices with their start and end apart: 7 -> 7, of which waited for: 4 -> 3; matrix products, arithmetic and copies ran while one was open for 0% -> 0% of each run, Pallas kernels for 17% -> 15%
where the time goes in v3:
time: 17.3 us; the launch traced here: 17 us
  starting transfers between devices  8.97 us (52%)
  Pallas kernels  3.61 us (21%)
  waiting for transfers between devices  2.97 us (17%)
  other arithmetic  0.8 us (5%)
  between operations  0.68 us (4%)
    ppermute x7, starting transfers between devices, swap(): return lax.ppermute(value, 'blk', [(i, i ^ mask) for i in range(count)])  8.97 us
    pallas_call x3, Pallas kernels, on_device(): total = add_call(*operands)  3.12 us
    ppermute x7, waiting for transfers between devices, swap(): return lax.ppermute(value, 'blk', [(i, i ^ mask) for i in range(count)])  2.97 us
    concatenate x1, other arithmetic, on_device(): own = lax.optimization_barrier(jnp.concatenate([points, vectors], axis=0))  0.72 us
    pallas_call x1, Pallas kernels, on_device(): scale, side, base, total = prepare_call(own, params)  0.49 us
  transfers between devices with their start and end apart: 7, of which 3 were waited for; matrix products, arithmetic and copies ran while one was open for 0% of the time, Pallas kernels for 15%

profile of v3, /device:TPU:0, one launch (start us, length us, event | category | flops | bytes accessed | tf_op | source)
XLA Modules:
  0.0 17.0 jit_solution(716833437249768500)
XLA Ops:
  0.0 0.7 %pad_maximum_fusion.2.own_ref = f32[16,256]{1,0:T(8,128)S(1)} fusion(f32[8,256]{1,0:T(8,128)} %param.5, f32[8,256]{1,0:T(8,128)} %param.4), kind=kLoop, calls=%fused_computation.2 | loop fusion | flops 4096 | bytes 32768 | tf_op jit(solution)/shard_map/concatenate | solution.py:125
  0.7 3.5 %collective-permute-start = (f32[16,256]{1,0:T(8,128)S(1)}, f32[16,256]{1,0:T(8,128)S(1)}, u32[]{:S(2)}, u32[]{:S(2)}) collective-permute-start(f32[16,256]{1,0:T(8,128)S(1)} %pad_maximum_fusion.2.own_ref), channel_id=1, source_target_pairs={{0,9},{1,8},{2,11},{3,10},{4,13},{5,12},{6,15},{7,14},{8,1},{9,0},... | collective-permute-start | bytes 49160 | tf_op jit(solution)/shard_map/ppermute | solution.py:129
  4.2 1.4 %collective-permute-done.rest_0_ = f32[16,256]{1,0:T(8,128)S(1)} collective-permute-done((f32[16,256]{1,0:T(8,128)S(1)}, f32[16,256]{1,0:T(8,128)S(1)}, u32[]{:S(2)}, u32[]{:S(2)}) %collective-permute-start) | collective-permute-done | bytes 16416 | tf_op jit(solution)/shard_map/ppermute | solution.py:129
  5.7 1.9 %collective-permute-start.1 = (f32[32,256]{1,0:T(8,128)S(1)}, f32[32,256]{1,0:T(8,128)S(1)}, u32[]{:S(2)}, u32[]{:S(2)}) collective-permute-start(f32[32,256]{1,0:T(8,128)S(1)} %pad_maximum_fusion.1), channel_id=1, source_target_pairs={{0,5},{1,4},{2,7},{3,6},{4,1},{5,0},{6,3},{7,2},{8,13},{9,12},{10,... | collective-permute-start | bytes 98312 | tf_op jit(solution)/shard_map/ppermute | solution.py:129
  8.2 0.0 copy-start
  8.2 1.6 %collective-permute-start.2 = (f32[32,256]{1,0:T(8,128)S(1)}, f32[32,256]{1,0:T(8,128)S(1)}, u32[]{:S(2)}, u32[]{:S(2)}) collective-permute-start(f32[32,256]{1,0:T(8,128)S(1)} %pad_maximum_fusion.1), channel_id=1, source_target_pairs={{0,3},{1,2},{2,1},{3,0},{4,7},{5,6},{6,5},{7,4},{8,11},{9,10},{10,... | collective-permute-start | bytes 98312 | tf_op jit(solution)/shard_map/ppermute | solution.py:129
  9.8 0.0 collective-permute-done.1.rest_1_
  9.8 1.1 %collective-permute-start.5 = (f32[32,256]{1,0:T(8,128)S(1)}, f32[32,256]{1,0:T(8,128)S(1)}, u32[]{:S(2)}, u32[]{:S(2)}) collective-permute-start(f32[32,256]{1,0:T(8,128)S(1)} %collective-permute-done.1.rest_1_), channel_id=1, source_target_pairs={{0,3},{1,2},{2,1},{3,0},{4,7},{5,6},{6,5},{7,4},{8,11},{9,10},{10,... | collective-permute-start | bytes 98312 | tf_op jit(solution)/shard_map/ppermute | solution.py:129
  10.9 0.4 %collective-permute-start.4 = (f32[64,256]{1,0:T(8,128)S(1)}, f32[64,256]{1,0:T(8,128)S(1)}, u32[]{:S(2)}, u32[]{:S(2)}) collective-permute-start(f32[64,256]{1,0:T(8,128)S(1)} %pad_maximum_fusion), channel_id=1, source_target_pairs={{0,1},{1,0},{2,3},{3,2},{4,5},{5,4},{6,7},{7,6},{8,9},{9,8},{10,11... | collective-permute-start | bytes 196616 | tf_op jit(solution)/shard_map/ppermute | solution.py:129
  11.3 0.3 %collective-permute-done.2.rest_2_ = f32[32,256]{1,0:T(8,128)S(1)} collective-permute-done((f32[32,256]{1,0:T(8,128)S(1)}, f32[32,256]{1,0:T(8,128)S(1)}, u32[]{:S(2)}, u32[]{:S(2)}) %collective-permute-start.2) | collective-permute-done | bytes 32800 | tf_op jit(solution)/shard_map/ppermute | solution.py:129
  11.6 0.4 %collective-permute-start.3 = (f32[32,256]{1,0:T(8,128)S(1)}, f32[32,256]{1,0:T(8,128)S(1)}, u32[]{:S(2)}, u32[]{:S(2)}) collective-permute-start(f32[32,256]{1,0:T(8,128)S(1)} %collective-permute-done.2.rest_2_), channel_id=1, source_target_pairs={{0,1},{1,0},{2,3},{3,2},{4,5},{5,4},{6,7},{7,6},{8,9},{9,8},{10,11... | collective-permute-start | bytes 98312 | tf_op jit(solution)/shard_map/ppermute | solution.py:129
  12.0 1.2 %collective-permute-done.5.rest_2_ = f32[32,256]{1,0:T(8,128)S(1)} collective-permute-done((f32[32,256]{1,0:T(8,128)S(1)}, f32[32,256]{1,0:T(8,128)S(1)}, u32[]{:S(2)}, u32[]{:S(2)}) %collective-permute-start.5) | collective-permute-done | bytes 32800 | tf_op jit(solution)/shard_map/ppermute | solution.py:129
  13.2 0.1 collective-permute-start.6
  13.3 0.0 copy-done
  13.3 0.1 pad_maximum_fusion.3.params_ref
  13.4 0.5 %prepare.1 = (f32[8,256]{1,0:T(8,128)S(1)}, bf16[64,256]{1,0:T(8,128)(2,1)S(1)}, f32[8,256]{1,0:T(8,128)S(1)}, f32[8,256]{1,0:T(8,128)S(1)}) custom-call(f32[16,256]{1,0:T(8,128)S(1)} %pad_maximum_fusion.2.own_ref, f32[9]{0:T(128)S(1)} %pad_maximum_fusion.3.params_ref), custom_call_target="tpu_custom_call" | custom-call | flops 100000 | bytes 16384 | tf_op jit(solution)/shard_map/prepare/pallas_call | solution.py:163
  13.9 0.8 %shard_map.46.acc_ref = f32[8,256]{1,0:T(8,128)S(1)} custom-call(f32[8,256]{1,0:T(8,128)S(1)} %get-tuple-element.9.scale_ref, bf16[64,256]{1,0:T(8,128)(2,1)S(1)} %get-tuple-element.10.side_ref, f32[8,256]{1,0:T(8,128)S(1)} %get-tuple-element.11.acc_ref, f32[16,256]{1,0:T(8,128)S(1)} %collective-permute-done.rest_0_, ...), custom_call_target="tpu_custom_call" | custom-call | flops 131072000 | bytes 81920 | tf_op jit(solution)/shard_map/pallas_call | solution.py:182
  14.7 0.0 collective-permute-done.3.rest_0_
  14.7 0.0 collective-permute-done.4.rest_1_
  14.7 1.2 %shard_map.47.acc_ref = f32[8,256]{1,0:T(8,128)S(1)} custom-call(f32[8,256]{1,0:T(8,128)S(1)} %get-tuple-element.9.scale_ref, bf16[64,256]{1,0:T(8,128)(2,1)S(1)} %get-tuple-element.10.side_ref, f32[8,256]{1,0:T(8,128)S(1)} %shard_map.46.acc_ref, f32[32,256]{1,0:T(8,128)S(1)} %collective-permute-done.3.rest_0_, ...), custom_call_target="tpu_custom_call" | custom-call | flops 209715200 | bytes 131072 | tf_op jit(solution)/shard_map/pallas_call | solution.py:182
  15.9 0.0 collective-permute-done.6.rest_1_
  15.9 1.1 %shard_map.48 = f32[8,256]{1,0:T(8,128)} custom-call(f32[8,256]{1,0:T(8,128)S(1)} %get-tuple-element.9.scale_ref, bf16[64,256]{1,0:T(8,128)(2,1)S(1)} %get-tuple-element.10.side_ref, f32[8,256]{1,0:T(8,128)S(1)} %shard_map.47.acc_ref, f32[8,256]{1,0:T(8,128)S(1)} %get-tuple-element.12.rest_0_, f32[32,256]{1,0:T(8,128)S(1)} %collective-permute-done.6.rest_1_), custom_call_target="tpu_custom_call" | custom-call | flops 52428800 | bytes 32768 | tf_op jit(solution)/shard_map/pallas_call | solution.py:182
  (2 shorter events, 0.0 us)
Async XLA Ops:
  0.7 4.9 %collective-permute-start = (f32[16,256]{1,0:T(8,128)S(1)}, f32[16,256]{1,0:T(8,128)S(1)}, u32[]{:S(2)}, u32[]{:S(2)}) collective-permute-start(f32[16,256]{1,0:T(8,128)S(1)} %pad_maximum_fusion.2.own_ref), channel_id=1, source_target_pairs={{0,9},{1,8},{2,11},{3,10},{4,13},{5,12},{6,15},{7,14},{8,1},{9,0},... | collective-permute-start | bytes 49160 | tf_op jit(solution)/shard_map/ppermute | solution.py:129
  5.7 4.1 %collective-permute-start.1 = (f32[32,256]{1,0:T(8,128)S(1)}, f32[32,256]{1,0:T(8,128)S(1)}, u32[]{:S(2)}, u32[]{:S(2)}) collective-permute-start(f32[32,256]{1,0:T(8,128)S(1)} %pad_maximum_fusion.1), channel_id=1, source_target_pairs={{0,5},{1,4},{2,7},{3,6},{4,1},{5,0},{6,3},{7,2},{8,13},{9,12},{10,... | collective-permute-start | bytes 98312 | tf_op jit(solution)/shard_map/ppermute | solution.py:129
  8.2 5.1 %copy-start = (f32[8]{0:T(128)S(1)}, f32[8]{0:T(128)}, u32[]{:S(2)}) copy-start(f32[8]{0:T(128)} %param.6) | copy-start | bytes 100
  8.2 3.4 %collective-permute-start.2 = (f32[32,256]{1,0:T(8,128)S(1)}, f32[32,256]{1,0:T(8,128)S(1)}, u32[]{:S(2)}, u32[]{:S(2)}) collective-permute-start(f32[32,256]{1,0:T(8,128)S(1)} %pad_maximum_fusion.1), channel_id=1, source_target_pairs={{0,3},{1,2},{2,1},{3,0},{4,7},{5,6},{6,5},{7,4},{8,11},{9,10},{10,... | collective-permute-start | bytes 98312 | tf_op jit(solution)/shard_map/ppermute | solution.py:129
  9.8 3.4 %collective-permute-start.5 = (f32[32,256]{1,0:T(8,128)S(1)}, f32[32,256]{1,0:T(8,128)S(1)}, u32[]{:S(2)}, u32[]{:S(2)}) collective-permute-start(f32[32,256]{1,0:T(8,128)S(1)} %collective-permute-done.1.rest_1_), channel_id=1, source_target_pairs={{0,3},{1,2},{2,1},{3,0},{4,7},{5,6},{6,5},{7,4},{8,11},{9,10},{10,... | collective-permute-start | bytes 98312 | tf_op jit(solution)/shard_map/ppermute | solution.py:129
  10.9 3.8 %collective-permute-start.4 = (f32[64,256]{1,0:T(8,128)S(1)}, f32[64,256]{1,0:T(8,128)S(1)}, u32[]{:S(2)}, u32[]{:S(2)}) collective-permute-start(f32[64,256]{1,0:T(8,128)S(1)} %pad_maximum_fusion), channel_id=1, source_target_pairs={{0,1},{1,0},{2,3},{3,2},{4,5},{5,4},{6,7},{7,6},{8,9},{9,8},{10,11... | collective-permute-start | bytes 196616 | tf_op jit(solution)/shard_map/ppermute | solution.py:129
  11.6 3.1 %collective-permute-start.3 = (f32[32,256]{1,0:T(8,128)S(1)}, f32[32,256]{1,0:T(8,128)S(1)}, u32[]{:S(2)}, u32[]{:S(2)}) collective-permute-start(f32[32,256]{1,0:T(8,128)S(1)} %collective-permute-done.2.rest_2_), channel_id=1, source_target_pairs={{0,1},{1,0},{2,3},{3,2},{4,5},{5,4},{6,7},{7,6},{8,9},{9,8},{10,11... | collective-permute-start | bytes 98312 | tf_op jit(solution)/shard_map/ppermute | solution.py:129
  13.2 2.7 %collective-permute-start.6 = (f32[32,256]{1,0:T(8,128)S(1)}, f32[32,256]{1,0:T(8,128)S(1)}, u32[]{:S(2)}, u32[]{:S(2)}) collective-permute-start(f32[32,256]{1,0:T(8,128)S(1)} %collective-permute-done.5.rest_2_), channel_id=1, source_target_pairs={{0,1},{1,0},{2,3},{3,2},{4,5},{5,4},{6,7},{7,6},{8,9},{9,8},{10,11... | collective-permute-start | bytes 98312 | tf_op jit(solution)/shard_map/ppermute | solution.py:129

commit v4 on v3

--- a/solution.py
+++ b/solution.py
@@ -101,7 +101,7 @@
     total = acc_ref[...]
     for piece_ref in rest:
         count = piece_ref.shape[0] // rows
-        group = math.gcd(count, 4)
+        group = count if count <= 8 else math.gcd(count, 8)
 
         def step(index, total, piece_ref=piece_ref, group=group):
             for k in range(group):
@@ -125,25 +125,26 @@
     own = lax.optimization_barrier(jnp.concatenate([points, vectors], axis=0))
     params = lax.optimization_barrier(jnp.concatenate([inv_length, noise]))
 
-    def swap(value, mask):
-        return lax.ppermute(value, "blk", [(i, i ^ mask) for i in range(count)])
+    def swap(value, masks):
+        pairs = [(i, i ^ masks[(i & 7).bit_count() % 2]) for i in range(count)]
+        return lax.ppermute(value, "blk", pairs)
 
     levels = count.bit_length() - 1
     if count != 1 << levels or levels < 3:
         others = [lax.ppermute(own, "blk", [(i, (i + k) % count) for i in range(count)]) for k in range(1, count)]
-        groups = [others + [newest, early], [early_core, near, late], [late_core]]
+        groups = [others + [newest, early, near_held], [near, late], [late_core]]
     else:
         held, others = own, []
         for bit in range(levels - 1, 2, -1):
-            others.append(swap(held, 1 << bit | 1))
+            others.append(swap(held, (1 << bit | 1,) * 2))
             held = jnp.concatenate([held, others[-1]], axis=0)
-        newest = swap(held, 5)
-        early = swap(held, 3)
-        late = swap(newest, 3)
-        near = swap(jnp.concatenate([held, newest], axis=0), 1)
-        early_core = swap(early, 1)
-        late_core = swap(late, 1)
-        groups = [others + [newest, early], [early_core, near, late], [late_core]]
+        newest = swap(held, (5, 3))
+        early = swap(held, (3, 5))
+        late = swap(newest, (3, 5))
+        near_held = swap(held, (1, 1))
+        near = swap(jnp.concatenate([newest, early], axis=0), (1, 1))
+        late_core = swap(late, (1, 1))
+        groups = [others + [newest, early, near_held], [near, late], [late_core]]
 
     side_rows = -(-(6 * dim + SUBLANES) // (2 * SUBLANES)) * 2 * SUBLANES
     prepare_call = pl.pallas_call(

time: 17.3 us -> 17.6 us (1.017)
  waiting for transfers between devices: 2.97 us -> 3.31 us
    ppermute x7, waiting for transfers between devices: 2.97 us -> 3.31 us  [swap(): return lax.ppermute(value, 'blk', pairs)]
  transfers between devices with their start and end apart: 7 -> 7, of which waited for: 3 -> 2; matrix products, arithmetic and copies ran while one was open for 0% -> 0% of each run, Pallas kernels for 15% -> 14%
where the time goes in v4:
time: 17.6 us; the launch traced here: 17.4 us
  starting transfers between devices  8.97 us (51%)
  Pallas kernels  3.59 us (20%)
  waiting for transfers between devices  3.31 us (19%)
  other arithmetic  0.8 us (5%)
  between operations  0.69 us (4%)
    ppermute x7, starting transfers between devices, swap(): return lax.ppermute(value, 'blk', pairs)  8.97 us
    ppermute x7, waiting for transfers between devices, swap(): return lax.ppermute(value, 'blk', pairs)  3.31 us
    pallas_call x3, Pallas kernels, on_device(): total = add_call(*operands)  3.1 us
    concatenate x1, other arithmetic, on_device(): own = lax.optimization_barrier(jnp.concatenate([points, vectors], axis=0))  0.72 us
    pallas_call x1, Pallas kernels, on_device(): scale, side, base, total = prepare_call(own, params)  0.49 us
  transfers between devices with their start and end apart: 7, of which 2 were waited for; matrix products, arithmetic and copies ran while one was open for 0% of the time, Pallas kernels for 14%

profile of v4, /device:TPU:0, one launch (start us, length us, event | category | flops | bytes accessed | tf_op | source)
XLA Modules:
  0.0 17.4 jit_solution(11039416071404911813)
XLA Ops:
  0.0 0.7 %pad_maximum_fusion.2.own_ref = f32[16,256]{1,0:T(8,128)S(1)} fusion(f32[8,256]{1,0:T(8,128)} %param.5, f32[8,256]{1,0:T(8,128)} %param.4), kind=kLoop, calls=%fused_computation.2 | loop fusion | flops 4096 | bytes 32768 | tf_op jit(solution)/shard_map/concatenate | solution.py:125
  0.7 3.5 %collective-permute-start = (f32[16,256]{1,0:T(8,128)S(1)}, f32[16,256]{1,0:T(8,128)S(1)}, u32[]{:S(2)}, u32[]{:S(2)}) collective-permute-start(f32[16,256]{1,0:T(8,128)S(1)} %pad_maximum_fusion.2.own_ref), channel_id=1, source_target_pairs={{0,9},{1,8},{2,11},{3,10},{4,13},{5,12},{6,15},{7,14},{8,1},{9,0},... | collective-permute-start | bytes 49160 | tf_op jit(solution)/shard_map/ppermute | solution.py:130
  4.2 1.4 %collective-permute-done.rest_0_ = f32[16,256]{1,0:T(8,128)S(1)} collective-permute-done((f32[16,256]{1,0:T(8,128)S(1)}, f32[16,256]{1,0:T(8,128)S(1)}, u32[]{:S(2)}, u32[]{:S(2)}) %collective-permute-start) | collective-permute-done | bytes 16416 | tf_op jit(solution)/shard_map/ppermute | solution.py:130
  5.7 1.9 %collective-permute-start.1 = (f32[32,256]{1,0:T(8,128)S(1)}, f32[32,256]{1,0:T(8,128)S(1)}, u32[]{:S(2)}, u32[]{:S(2)}) collective-permute-start(f32[32,256]{1,0:T(8,128)S(1)} %pad_maximum_fusion.1), channel_id=1, source_target_pairs={{0,5},{1,2},{2,1},{3,6},{4,7},{5,0},{6,3},{7,4},{8,13},{9,10},{10,... | collective-permute-start | bytes 98312 | tf_op jit(solution)/shard_map/ppermute | solution.py:130
  7.6 1.5 %collective-permute-start.2 = (f32[32,256]{1,0:T(8,128)S(1)}, f32[32,256]{1,0:T(8,128)S(1)}, u32[]{:S(2)}, u32[]{:S(2)}) collective-permute-start(f32[32,256]{1,0:T(8,128)S(1)} %pad_maximum_fusion.1), channel_id=1, source_target_pairs={{0,3},{1,4},{2,7},{3,0},{4,1},{5,6},{6,5},{7,2},{8,11},{9,12},{10,... | collective-permute-start | bytes 98312 | tf_op jit(solution)/shard_map/ppermute | solution.py:130
  9.7 0.0 copy-start
  9.7 0.2 %collective-permute-start.3 = (f32[32,256]{1,0:T(8,128)S(1)}, f32[32,256]{1,0:T(8,128)S(1)}, u32[]{:S(2)}, u32[]{:S(2)}) collective-permute-start(f32[32,256]{1,0:T(8,128)S(1)} %pad_maximum_fusion.1), channel_id=1, source_target_pairs={{0,1},{1,0},{2,3},{3,2},{4,5},{5,4},{6,7},{7,6},{8,9},{9,8},{10,11... | collective-permute-start | bytes 98312 | tf_op jit(solution)/shard_map/ppermute | solution.py:130
  9.9 0.0 collective-permute-done.1.rest_1_
  9.9 1.3 %collective-permute-start.5 = (f32[32,256]{1,0:T(8,128)S(1)}, f32[32,256]{1,0:T(8,128)S(1)}, u32[]{:S(2)}, u32[]{:S(2)}) collective-permute-start(f32[32,256]{1,0:T(8,128)S(1)} %collective-permute-done.1.rest_1_), channel_id=1, source_target_pairs={{0,3},{1,4},{2,7},{3,0},{4,1},{5,6},{6,5},{7,2},{8,11},{9,12},{10,... | collective-permute-start | bytes 98312 | tf_op jit(solution)/shard_map/ppermute | solution.py:130
  11.2 0.0 collective-permute-done.2.rest_2_
  11.2 0.2 collective-permute-start.4
  11.4 1.8 %collective-permute-done.5.rest_1_ = f32[32,256]{1,0:T(8,128)S(1)} collective-permute-done((f32[32,256]{1,0:T(8,128)S(1)}, f32[32,256]{1,0:T(8,128)S(1)}, u32[]{:S(2)}, u32[]{:S(2)}) %collective-permute-start.5) | collective-permute-done | bytes 32800 | tf_op jit(solution)/shard_map/ppermute | solution.py:130
  13.3 0.4 %collective-permute-start.6 = (f32[32,256]{1,0:T(8,128)S(1)}, f32[32,256]{1,0:T(8,128)S(1)}, u32[]{:S(2)}, u32[]{:S(2)}) collective-permute-start(f32[32,256]{1,0:T(8,128)S(1)} %collective-permute-done.5.rest_1_), channel_id=1, source_target_pairs={{0,1},{1,0},{2,3},{3,2},{4,5},{5,4},{6,7},{7,6},{8,9},{9,8},{10,11... | collective-permute-start | bytes 98312 | tf_op jit(solution)/shard_map/ppermute | solution.py:130
  13.7 0.0 copy-done
  13.7 0.1 pad_maximum_fusion.3.params_ref
  13.7 0.5 %prepare.1 = (f32[8,256]{1,0:T(8,128)S(1)}, bf16[64,256]{1,0:T(8,128)(2,1)S(1)}, f32[8,256]{1,0:T(8,128)S(1)}, f32[8,256]{1,0:T(8,128)S(1)}) custom-call(f32[16,256]{1,0:T(8,128)S(1)} %pad_maximum_fusion.2.own_ref, f32[9]{0:T(128)S(1)} %pad_maximum_fusion.3.params_ref), custom_call_target="tpu_custom_call" | custom-call | flops 100000 | bytes 16384 | tf_op jit(solution)/shard_map/prepare/pallas_call | solution.py:164
  14.2 0.0 collective-permute-done.3.rest_3_
  14.2 1.0 %shard_map.46.acc_ref = f32[8,256]{1,0:T(8,128)S(1)} custom-call(f32[8,256]{1,0:T(8,128)S(1)} %get-tuple-element.9.scale_ref, bf16[64,256]{1,0:T(8,128)(2,1)S(1)} %get-tuple-element.10.side_ref, f32[8,256]{1,0:T(8,128)S(1)} %get-tuple-element.11.acc_ref, f32[16,256]{1,0:T(8,128)S(1)} %collective-permute-done.rest_0_, ...), custom_call_target="tpu_custom_call" | custom-call | flops 183500800 | bytes 114688 | tf_op jit(solution)/shard_map/pallas_call | solution.py:183
  15.3 0.0 collective-permute-done.4.rest_0_
  15.3 0.9 %shard_map.47.acc_ref = f32[8,256]{1,0:T(8,128)S(1)} custom-call(f32[8,256]{1,0:T(8,128)S(1)} %get-tuple-element.9.scale_ref, bf16[64,256]{1,0:T(8,128)(2,1)S(1)} %get-tuple-element.10.side_ref, f32[8,256]{1,0:T(8,128)S(1)} %shard_map.46.acc_ref, f32[64,256]{1,0:T(8,128)S(1)} %collective-permute-done.4.rest_0_, f32[32,256]{1,0:T(8,128)S(1)} %collective-permute-done.5.rest_1_), custom_call_target="tpu_custom_call" | custom-call | flops 157286400 | bytes 98304 | tf_op jit(solution)/shard_map/pallas_call | solution.py:183
  16.2 0.0 collective-permute-done.6.rest_1_
  16.2 1.1 %shard_map.48 = f32[8,256]{1,0:T(8,128)} custom-call(f32[8,256]{1,0:T(8,128)S(1)} %get-tuple-element.9.scale_ref, bf16[64,256]{1,0:T(8,128)(2,1)S(1)} %get-tuple-element.10.side_ref, f32[8,256]{1,0:T(8,128)S(1)} %shard_map.47.acc_ref, f32[8,256]{1,0:T(8,128)S(1)} %get-tuple-element.12.rest_0_, f32[32,256]{1,0:T(8,128)S(1)} %collective-permute-done.6.rest_1_), custom_call_target="tpu_custom_call" | custom-call | flops 52428800 | bytes 32768 | tf_op jit(solution)/shard_map/pallas_call | solution.py:183
  (2 shorter events, 0.0 us)
Async XLA Ops:
  0.7 4.9 %collective-permute-start = (f32[16,256]{1,0:T(8,128)S(1)}, f32[16,256]{1,0:T(8,128)S(1)}, u32[]{:S(2)}, u32[]{:S(2)}) collective-permute-start(f32[16,256]{1,0:T(8,128)S(1)} %pad_maximum_fusion.2.own_ref), channel_id=1, source_target_pairs={{0,9},{1,8},{2,11},{3,10},{4,13},{5,12},{6,15},{7,14},{8,1},{9,0},... | collective-permute-start | bytes 49160 | tf_op jit(solution)/shard_map/ppermute | solution.py:130
  5.7 4.3 %collective-permute-start.1 = (f32[32,256]{1,0:T(8,128)S(1)}, f32[32,256]{1,0:T(8,128)S(1)}, u32[]{:S(2)}, u32[]{:S(2)}) collective-permute-start(f32[32,256]{1,0:T(8,128)S(1)} %pad_maximum_fusion.1), channel_id=1, source_target_pairs={{0,5},{1,2},{2,1},{3,6},{4,7},{5,0},{6,3},{7,4},{8,13},{9,10},{10,... | collective-permute-start | bytes 98312 | tf_op jit(solution)/shard_map/ppermute | solution.py:130
  7.6 3.7 %collective-permute-start.2 = (f32[32,256]{1,0:T(8,128)S(1)}, f32[32,256]{1,0:T(8,128)S(1)}, u32[]{:S(2)}, u32[]{:S(2)}) collective-permute-start(f32[32,256]{1,0:T(8,128)S(1)} %pad_maximum_fusion.1), channel_id=1, source_target_pairs={{0,3},{1,4},{2,7},{3,0},{4,1},{5,6},{6,5},{7,2},{8,11},{9,12},{10,... | collective-permute-start | bytes 98312 | tf_op jit(solution)/shard_map/ppermute | solution.py:130
  9.7 3.9 %copy-start = (f32[8]{0:T(128)S(1)}, f32[8]{0:T(128)}, u32[]{:S(2)}) copy-start(f32[8]{0:T(128)} %param.6) | copy-start | bytes 100
  9.7 4.5 %collective-permute-start.3 = (f32[32,256]{1,0:T(8,128)S(1)}, f32[32,256]{1,0:T(8,128)S(1)}, u32[]{:S(2)}, u32[]{:S(2)}) collective-permute-start(f32[32,256]{1,0:T(8,128)S(1)} %pad_maximum_fusion.1), channel_id=1, source_target_pairs={{0,1},{1,0},{2,3},{3,2},{4,5},{5,4},{6,7},{7,6},{8,9},{9,8},{10,11... | collective-permute-start | bytes 98312 | tf_op jit(solution)/shard_map/ppermute | solution.py:130
  9.9 3.3 %collective-permute-start.5 = (f32[32,256]{1,0:T(8,128)S(1)}, f32[32,256]{1,0:T(8,128)S(1)}, u32[]{:S(2)}, u32[]{:S(2)}) collective-permute-start(f32[32,256]{1,0:T(8,128)S(1)} %collective-permute-done.1.rest_1_), channel_id=1, source_target_pairs={{0,3},{1,4},{2,7},{3,0},{4,1},{5,6},{6,5},{7,2},{8,11},{9,12},{10,... | collective-permute-start | bytes 98312 | tf_op jit(solution)/shard_map/ppermute | solution.py:130
  11.2 4.0 %collective-permute-start.4 = (f32[64,256]{1,0:T(8,128)S(1)}, f32[64,256]{1,0:T(8,128)S(1)}, u32[]{:S(2)}, u32[]{:S(2)}) collective-permute-start(f32[64,256]{1,0:T(8,128)S(1)} %pad_maximum_fusion), channel_id=1, source_target_pairs={{0,1},{1,0},{2,3},{3,2},{4,5},{5,4},{6,7},{7,6},{8,9},{9,8},{10,11... | collective-permute-start | bytes 196616 | tf_op jit(solution)/shard_map/ppermute | solution.py:130
  13.3 3.0 %collective-permute-start.6 = (f32[32,256]{1,0:T(8,128)S(1)}, f32[32,256]{1,0:T(8,128)S(1)}, u32[]{:S(2)}, u32[]{:S(2)}) collective-permute-start(f32[32,256]{1,0:T(8,128)S(1)} %collective-permute-done.5.rest_1_), channel_id=1, source_target_pairs={{0,1},{1,0},{2,3},{3,2},{4,5},{5,4},{6,7},{7,6},{8,9},{9,8},{10,11... | collective-permute-start | bytes 98312 | tf_op jit(solution)/shard_map/ppermute | solution.py:130

commit v5 on v3

--- a/solution.py
+++ b/solution.py
@@ -101,7 +101,7 @@
     total = acc_ref[...]
     for piece_ref in rest:
         count = piece_ref.shape[0] // rows
-        group = math.gcd(count, 4)
+        group = count if count <= 8 else math.gcd(count, 8)
 
         def step(index, total, piece_ref=piece_ref, group=group):
             for k in range(group):
@@ -130,20 +130,20 @@
 
     levels = count.bit_length() - 1
     if count != 1 << levels or levels < 3:
-        others = [lax.ppermute(own, "blk", [(i, (i + k) % count) for i in range(count)]) for k in range(1, count)]
-        groups = [others + [newest, early], [early_core, near, late], [late_core]]
+        turns = [[(i, (i + k) % count) for i in range(count)] for k in range(1, count)]
+        groups = [[lax.ppermute(own, "blk", pairs) for pairs in turns]]
     else:
         held, others = own, []
         for bit in range(levels - 1, 2, -1):
             others.append(swap(held, 1 << bit | 1))
             held = jnp.concatenate([held, others[-1]], axis=0)
-        newest = swap(held, 5)
-        early = swap(held, 3)
-        late = swap(newest, 3)
-        near = swap(jnp.concatenate([held, newest], axis=0), 1)
-        early_core = swap(early, 1)
+        newest = swap(held, 3)
+        early = swap(held, 5)
+        late = swap(newest, 5)
+        near_held = swap(held, 1)
+        near = swap(jnp.concatenate([newest, early], axis=0), 1)
         late_core = swap(late, 1)
-        groups = [others + [newest, early], [early_core, near, late], [late_core]]
+        groups = [others + [newest, early, near_held], [near, late], [late_core]]
 
     side_rows = -(-(6 * dim + SUBLANES) // (2 * SUBLANES)) * 2 * SUBLANES
     prepare_call = pl.pallas_call(

time: 17.3 us -> 17.6 us (1.017)
  waiting for transfers between devices: 2.97 us -> 3.31 us
    ppermute x7, waiting for transfers between devices: 2.97 us -> 3.31 us  [swap(): return lax.ppermute(value, 'blk', [(i, i ^ mask) for i in range(count)])]
  transfers between devices with their start and end apart: 7 -> 7, of which waited for: 3 -> 2; matrix products, arithmetic and copies ran while one was open for 0% -> 0% of each run, Pallas kernels for 15% -> 14%
where the time goes in v5:
time: 17.6 us; the launch traced here: 17.4 us
  starting transfers between devices  8.97 us (51%)
  Pallas kernels  3.59 us (20%)
  waiting for transfers between devices  3.31 us (19%)
  other arithmetic  0.8 us (5%)
  between operations  0.69 us (4%)
    ppermute x7, starting transfers between devices, swap(): return lax.ppermute(value, 'blk', [(i, i ^ mask) for i in range(count)])  8.97 us
    ppermute x7, waiting for transfers between devices, swap(): return lax.ppermute(value, 'blk', [(i, i ^ mask) for i in range(count)])  3.31 us
    pallas_call x3, Pallas kernels, on_device(): total = add_call(*operands)  3.1 us
    concatenate x1, other arithmetic, on_device(): own = lax.optimization_barrier(jnp.concatenate([points, vectors], axis=0))  0.72 us
    pallas_call x1, Pallas kernels, on_device(): scale, side, base, total = prepare_call(own, params)  0.49 us
  transfers between devices with their start and end apart: 7, of which 2 were waited for; matrix products, arithmetic and copies ran while one was open for 0% of the time, Pallas kernels for 14%

profile of v5, /device:TPU:0, one launch (start us, length us, event | category | flops | bytes accessed | tf_op | source)
XLA Modules:
  0.0 17.4 jit_solution(800402711758138577)
XLA Ops:
  0.0 0.7 %pad_maximum_fusion.2.own_ref = f32[16,256]{1,0:T(8,128)S(1)} fusion(f32[8,256]{1,0:T(8,128)} %param.5, f32[8,256]{1,0:T(8,128)} %param.4), kind=kLoop, calls=%fused_computation.2 | loop fusion | flops 4096 | bytes 32768 | tf_op jit(solution)/shard_map/concatenate | solution.py:125
  0.7 3.5 %collective-permute-start = (f32[16,256]{1,0:T(8,128)S(1)}, f32[16,256]{1,0:T(8,128)S(1)}, u32[]{:S(2)}, u32[]{:S(2)}) collective-permute-start(f32[16,256]{1,0:T(8,128)S(1)} %pad_maximum_fusion.2.own_ref), channel_id=1, source_target_pairs={{0,9},{1,8},{2,11},{3,10},{4,13},{5,12},{6,15},{7,14},{8,1},{9,0},... | collective-permute-start | bytes 49160 | tf_op jit(solution)/shard_map/ppermute | solution.py:129
  4.2 1.4 %collective-permute-done.rest_0_ = f32[16,256]{1,0:T(8,128)S(1)} collective-permute-done((f32[16,256]{1,0:T(8,128)S(1)}, f32[16,256]{1,0:T(8,128)S(1)}, u32[]{:S(2)}, u32[]{:S(2)}) %collective-permute-start) | collective-permute-done | bytes 16416 | tf_op jit(solution)/shard_map/ppermute | solution.py:129
  5.7 1.8 %collective-permute-start.1 = (f32[32,256]{1,0:T(8,128)S(1)}, f32[32,256]{1,0:T(8,128)S(1)}, u32[]{:S(2)}, u32[]{:S(2)}) collective-permute-start(f32[32,256]{1,0:T(8,128)S(1)} %pad_maximum_fusion.1), channel_id=1, source_target_pairs={{0,3},{1,2},{2,1},{3,0},{4,7},{5,6},{6,5},{7,4},{8,11},{9,10},{10,... | collective-permute-start | bytes 98312 | tf_op jit(solution)/shard_map/ppermute | solution.py:129
  7.5 1.6 %collective-permute-start.2 = (f32[32,256]{1,0:T(8,128)S(1)}, f32[32,256]{1,0:T(8,128)S(1)}, u32[]{:S(2)}, u32[]{:S(2)}) collective-permute-start(f32[32,256]{1,0:T(8,128)S(1)} %pad_maximum_fusion.1), channel_id=1, source_target_pairs={{0,5},{1,4},{2,7},{3,6},{4,1},{5,0},{6,3},{7,2},{8,13},{9,12},{10,... | collective-permute-start | bytes 98312 | tf_op jit(solution)/shard_map/ppermute | solution.py:129
  9.7 0.0 copy-start
  9.7 0.2 %collective-permute-start.3 = (f32[32,256]{1,0:T(8,128)S(1)}, f32[32,256]{1,0:T(8,128)S(1)}, u32[]{:S(2)}, u32[]{:S(2)}) collective-permute-start(f32[32,256]{1,0:T(8,128)S(1)} %pad_maximum_fusion.1), channel_id=1, source_target_pairs={{0,1},{1,0},{2,3},{3,2},{4,5},{5,4},{6,7},{7,6},{8,9},{9,8},{10,11... | collective-permute-start | bytes 98312 | tf_op jit(solution)/shard_map/ppermute | solution.py:129
  9.9 0.0 collective-permute-done.1.rest_1_
  9.9 1.0 %collective-permute-start.5 = (f32[32,256]{1,0:T(8,128)S(1)}, f32[32,256]{1,0:T(8,128)S(1)}, u32[]{:S(2)}, u32[]{:S(2)}) collective-permute-start(f32[32,256]{1,0:T(8,128)S(1)} %collective-permute-done.1.rest_1_), channel_id=1, source_target_pairs={{0,5},{1,4},{2,7},{3,6},{4,1},{5,0},{6,3},{7,2},{8,13},{9,12},{10,... | collective-permute-start | bytes 98312 | tf_op jit(solution)/shard_map/ppermute | solution.py:129
  11.0 0.0 collective-permute-done.2.rest_2_
  11.0 0.5 %collective-permute-start.4 = (f32[64,256]{1,0:T(8,128)S(1)}, f32[64,256]{1,0:T(8,128)S(1)}, u32[]{:S(2)}, u32[]{:S(2)}) collective-permute-start(f32[64,256]{1,0:T(8,128)S(1)} %pad_maximum_fusion), channel_id=1, source_target_pairs={{0,1},{1,0},{2,3},{3,2},{4,5},{5,4},{6,7},{7,6},{8,9},{9,8},{10,11... | collective-permute-start | bytes 196616 | tf_op jit(solution)/shard_map/ppermute | solution.py:129
  11.4 1.8 %collective-permute-done.5.rest_1_ = f32[32,256]{1,0:T(8,128)S(1)} collective-permute-done((f32[32,256]{1,0:T(8,128)S(1)}, f32[32,256]{1,0:T(8,128)S(1)}, u32[]{:S(2)}, u32[]{:S(2)}) %collective-permute-start.5) | collective-permute-done | bytes 32800 | tf_op jit(solution)/shard_map/ppermute | solution.py:129
  13.3 0.4 %collective-permute-start.6 = (f32[32,256]{1,0:T(8,128)S(1)}, f32[32,256]{1,0:T(8,128)S(1)}, u32[]{:S(2)}, u32[]{:S(2)}) collective-permute-start(f32[32,256]{1,0:T(8,128)S(1)} %collective-permute-done.5.rest_1_), channel_id=1, source_target_pairs={{0,1},{1,0},{2,3},{3,2},{4,5},{5,4},{6,7},{7,6},{8,9},{9,8},{10,11... | collective-permute-start | bytes 98312 | tf_op jit(solution)/shard_map/ppermute | solution.py:129
  13.7 0.0 copy-done
  13.7 0.1 pad_maximum_fusion.3.params_ref
  13.7 0.5 %prepare.1 = (f32[8,256]{1,0:T(8,128)S(1)}, bf16[64,256]{1,0:T(8,128)(2,1)S(1)}, f32[8,256]{1,0:T(8,128)S(1)}, f32[8,256]{1,0:T(8,128)S(1)}) custom-call(f32[16,256]{1,0:T(8,128)S(1)} %pad_maximum_fusion.2.own_ref, f32[9]{0:T(128)S(1)} %pad_maximum_fusion.3.params_ref), custom_call_target="tpu_custom_call" | custom-call | flops 100000 | bytes 16384 | tf_op jit(solution)/shard_map/prepare/pallas_call | solution.py:163
  14.2 0.0 collective-permute-done.3.rest_3_
  14.2 1.0 %shard_map.46.acc_ref = f32[8,256]{1,0:T(8,128)S(1)} custom-call(f32[8,256]{1,0:T(8,128)S(1)} %get-tuple-element.9.scale_ref, bf16[64,256]{1,0:T(8,128)(2,1)S(1)} %get-tuple-element.10.side_ref, f32[8,256]{1,0:T(8,128)S(1)} %get-tuple-element.11.acc_ref, f32[16,256]{1,0:T(8,128)S(1)} %collective-permute-done.rest_0_, ...), custom_call_target="tpu_custom_call" | custom-call | flops 183500800 | bytes 114688 | tf_op jit(solution)/shard_map/pallas_call | solution.py:182
  15.3 0.0 collective-permute-done.4.rest_0_
  15.3 0.9 %shard_map.47.acc_ref = f32[8,256]{1,0:T(8,128)S(1)} custom-call(f32[8,256]{1,0:T(8,128)S(1)} %get-tuple-element.9.scale_ref, bf16[64,256]{1,0:T(8,128)(2,1)S(1)} %get-tuple-element.10.side_ref, f32[8,256]{1,0:T(8,128)S(1)} %shard_map.46.acc_ref, f32[64,256]{1,0:T(8,128)S(1)} %collective-permute-done.4.rest_0_, f32[32,256]{1,0:T(8,128)S(1)} %collective-permute-done.5.rest_1_), custom_call_target="tpu_custom_call" | custom-call | flops 157286400 | bytes 98304 | tf_op jit(solution)/shard_map/pallas_call | solution.py:182
  16.2 0.0 collective-permute-done.6.rest_1_
  16.2 1.1 %shard_map.48 = f32[8,256]{1,0:T(8,128)} custom-call(f32[8,256]{1,0:T(8,128)S(1)} %get-tuple-element.9.scale_ref, bf16[64,256]{1,0:T(8,128)(2,1)S(1)} %get-tuple-element.10.side_ref, f32[8,256]{1,0:T(8,128)S(1)} %shard_map.47.acc_ref, f32[8,256]{1,0:T(8,128)S(1)} %get-tuple-element.12.rest_0_, f32[32,256]{1,0:T(8,128)S(1)} %collective-permute-done.6.rest_1_), custom_call_target="tpu_custom_call" | custom-call | flops 52428800 | bytes 32768 | tf_op jit(solution)/shard_map/pallas_call | solution.py:182
  (2 shorter events, 0.0 us)
Async XLA Ops:
  0.7 4.9 %collective-permute-start = (f32[16,256]{1,0:T(8,128)S(1)}, f32[16,256]{1,0:T(8,128)S(1)}, u32[]{:S(2)}, u32[]{:S(2)}) collective-permute-start(f32[16,256]{1,0:T(8,128)S(1)} %pad_maximum_fusion.2.own_ref), channel_id=1, source_target_pairs={{0,9},{1,8},{2,11},{3,10},{4,13},{5,12},{6,15},{7,14},{8,1},{9,0},... | collective-permute-start | bytes 49160 | tf_op jit(solution)/shard_map/ppermute | solution.py:129
  5.7 4.3 %collective-permute-start.1 = (f32[32,256]{1,0:T(8,128)S(1)}, f32[32,256]{1,0:T(8,128)S(1)}, u32[]{:S(2)}, u32[]{:S(2)}) collective-permute-start(f32[32,256]{1,0:T(8,128)S(1)} %pad_maximum_fusion.1), channel_id=1, source_target_pairs={{0,3},{1,2},{2,1},{3,0},{4,7},{5,6},{6,5},{7,4},{8,11},{9,10},{10,... | collective-permute-start | bytes 98312 | tf_op jit(solution)/shard_map/ppermute | solution.py:129
  7.5 3.5 %collective-permute-start.2 = (f32[32,256]{1,0:T(8,128)S(1)}, f32[32,256]{1,0:T(8,128)S(1)}, u32[]{:S(2)}, u32[]{:S(2)}) collective-permute-start(f32[32,256]{1,0:T(8,128)S(1)} %pad_maximum_fusion.1), channel_id=1, source_target_pairs={{0,5},{1,4},{2,7},{3,6},{4,1},{5,0},{6,3},{7,2},{8,13},{9,12},{10,... | collective-permute-start | bytes 98312 | tf_op jit(solution)/shard_map/ppermute | solution.py:129
  9.7 3.9 %copy-start = (f32[8]{0:T(128)S(1)}, f32[8]{0:T(128)}, u32[]{:S(2)}) copy-start(f32[8]{0:T(128)} %param.6) | copy-start | bytes 100
  9.7 4.5 %collective-permute-start.3 = (f32[32,256]{1,0:T(8,128)S(1)}, f32[32,256]{1,0:T(8,128)S(1)}, u32[]{:S(2)}, u32[]{:S(2)}) collective-permute-start(f32[32,256]{1,0:T(8,128)S(1)} %pad_maximum_fusion.1), channel_id=1, source_target_pairs={{0,1},{1,0},{2,3},{3,2},{4,5},{5,4},{6,7},{7,6},{8,9},{9,8},{10,11... | collective-permute-start | bytes 98312 | tf_op jit(solution)/shard_map/ppermute | solution.py:129
  9.9 3.3 %collective-permute-start.5 = (f32[32,256]{1,0:T(8,128)S(1)}, f32[32,256]{1,0:T(8,128)S(1)}, u32[]{:S(2)}, u32[]{:S(2)}) collective-permute-start(f32[32,256]{1,0:T(8,128)S(1)} %collective-permute-done.1.rest_1_), channel_id=1, source_target_pairs={{0,5},{1,4},{2,7},{3,6},{4,1},{5,0},{6,3},{7,2},{8,13},{9,12},{10,... | collective-permute-start | bytes 98312 | tf_op jit(solution)/shard_map/ppermute | solution.py:129
  11.0 4.3 %collective-permute-start.4 = (f32[64,256]{1,0:T(8,128)S(1)}, f32[64,256]{1,0:T(8,128)S(1)}, u32[]{:S(2)}, u32[]{:S(2)}) collective-permute-start(f32[64,256]{1,0:T(8,128)S(1)} %pad_maximum_fusion), channel_id=1, source_target_pairs={{0,1},{1,0},{2,3},{3,2},{4,5},{5,4},{6,7},{7,6},{8,9},{9,8},{10,11... | collective-permute-start | bytes 196616 | tf_op jit(solution)/shard_map/ppermute | solution.py:129
  13.3 3.0 %collective-permute-start.6 = (f32[32,256]{1,0:T(8,128)S(1)}, f32[32,256]{1,0:T(8,128)S(1)}, u32[]{:S(2)}, u32[]{:S(2)}) collective-permute-start(f32[32,256]{1,0:T(8,128)S(1)} %collective-permute-done.5.rest_1_), channel_id=1, source_target_pairs={{0,1},{1,0},{2,3},{3,2},{4,5},{5,4},{6,7},{7,6},{8,9},{9,8},{10,11... | collective-permute-start | bytes 98312 | tf_op jit(solution)/shard_map/ppermute | solution.py:129

commit v6 on v5

--- a/solution.py
+++ b/solution.py
@@ -134,12 +134,12 @@
         groups = [[lax.ppermute(own, "blk", pairs) for pairs in turns]]
     else:
         held, others = own, []
-        for bit in range(levels - 1, 2, -1):
-            others.append(swap(held, 1 << bit | 1))
+        for _ in range(levels - 1, 2, -1):
+            others.append(swap(held, 9))
             held = jnp.concatenate([held, others[-1]], axis=0)
-        newest = swap(held, 3)
-        early = swap(held, 5)
-        late = swap(newest, 5)
+        newest = swap(held, 5)
+        early = swap(held, 3)
+        late = swap(newest, 3)
         near_held = swap(held, 1)
         near = swap(jnp.concatenate([newest, early], axis=0), 1)
         late_core = swap(late, 1)

time: 17.6 us -> 17.6 us (level)
  no operation moved by 1% of the time
where the time goes in v6:
time: 17.6 us; the launch traced here: 17.4 us
  starting transfers between devices  8.92 us (51%)
  Pallas kernels  3.59 us (20%)
  waiting for transfers between devices  3.37 us (19%)
  other arithmetic  0.8 us (5%)
  between operations  0.69 us (4%)
    ppermute x7, starting transfers between devices, swap(): return lax.ppermute(value, 'blk', [(i, i ^ mask) for i in range(count)])  8.92 us
    ppermute x7, waiting for transfers between devices, swap(): return lax.ppermute(value, 'blk', [(i, i ^ mask) for i in range(count)])  3.37 us
    pallas_call x3, Pallas kernels, on_device(): total = add_call(*operands)  3.1 us
    concatenate x1, other arithmetic, on_device(): own = lax.optimization_barrier(jnp.concatenate([points, vectors], axis=0))  0.72 us
    pallas_call x1, Pallas kernels, on_device(): scale, side, base, total = prepare_call(own, params)  0.49 us
  transfers between devices with their start and end apart: 7, of which 2 were waited for; matrix products, arithmetic and copies ran while one was open for 0% of the time, Pallas kernels for 14%

profile of v6, /device:TPU:0, one launch (start us, length us, event | category | flops | bytes accessed | tf_op | source)
XLA Modules:
  0.0 17.4 jit_solution(11628580622776620404)
XLA Ops:
  0.0 0.7 %pad_maximum_fusion.2.own_ref = f32[16,256]{1,0:T(8,128)S(1)} fusion(f32[8,256]{1,0:T(8,128)} %param.5, f32[8,256]{1,0:T(8,128)} %param.4), kind=kLoop, calls=%fused_computation.2 | loop fusion | flops 4096 | bytes 32768 | tf_op jit(solution)/shard_map/concatenate | solution.py:125
  0.7 3.5 %collective-permute-start = (f32[16,256]{1,0:T(8,128)S(1)}, f32[16,256]{1,0:T(8,128)S(1)}, u32[]{:S(2)}, u32[]{:S(2)}) collective-permute-start(f32[16,256]{1,0:T(8,128)S(1)} %pad_maximum_fusion.2.own_ref), channel_id=1, source_target_pairs={{0,9},{1,8},{2,11},{3,10},{4,13},{5,12},{6,15},{7,14},{8,1},{9,0},... | collective-permute-start | bytes 49160 | tf_op jit(solution)/shard_map/ppermute | solution.py:129
  4.2 1.4 %collective-permute-done.rest_0_ = f32[16,256]{1,0:T(8,128)S(1)} collective-permute-done((f32[16,256]{1,0:T(8,128)S(1)}, f32[16,256]{1,0:T(8,128)S(1)}, u32[]{:S(2)}, u32[]{:S(2)}) %collective-permute-start) | collective-permute-done | bytes 16416 | tf_op jit(solution)/shard_map/ppermute | solution.py:129
  5.7 1.9 %collective-permute-start.1 = (f32[32,256]{1,0:T(8,128)S(1)}, f32[32,256]{1,0:T(8,128)S(1)}, u32[]{:S(2)}, u32[]{:S(2)}) collective-permute-start(f32[32,256]{1,0:T(8,128)S(1)} %pad_maximum_fusion.1), channel_id=1, source_target_pairs={{0,5},{1,4},{2,7},{3,6},{4,1},{5,0},{6,3},{7,2},{8,13},{9,12},{10,... | collective-permute-start | bytes 98312 | tf_op jit(solution)/shard_map/ppermute | solution.py:129
  7.6 1.5 %collective-permute-start.2 = (f32[32,256]{1,0:T(8,128)S(1)}, f32[32,256]{1,0:T(8,128)S(1)}, u32[]{:S(2)}, u32[]{:S(2)}) collective-permute-start(f32[32,256]{1,0:T(8,128)S(1)} %pad_maximum_fusion.1), channel_id=1, source_target_pairs={{0,3},{1,2},{2,1},{3,0},{4,7},{5,6},{6,5},{7,4},{8,11},{9,10},{10,... | collective-permute-start | bytes 98312 | tf_op jit(solution)/shard_map/ppermute | solution.py:129
  9.7 0.0 copy-start
  9.7 0.2 %collective-permute-start.3 = (f32[32,256]{1,0:T(8,128)S(1)}, f32[32,256]{1,0:T(8,128)S(1)}, u32[]{:S(2)}, u32[]{:S(2)}) collective-permute-start(f32[32,256]{1,0:T(8,128)S(1)} %pad_maximum_fusion.1), channel_id=1, source_target_pairs={{0,1},{1,0},{2,3},{3,2},{4,5},{5,4},{6,7},{7,6},{8,9},{9,8},{10,11... | collective-permute-start | bytes 98312 | tf_op jit(solution)/shard_map/ppermute | solution.py:129
  9.9 0.0 collective-permute-done.1.rest_1_
  9.9 1.0 %collective-permute-start.5 = (f32[32,256]{1,0:T(8,128)S(1)}, f32[32,256]{1,0:T(8,128)S(1)}, u32[]{:S(2)}, u32[]{:S(2)}) collective-permute-start(f32[32,256]{1,0:T(8,128)S(1)} %collective-permute-done.1.rest_1_), channel_id=1, source_target_pairs={{0,3},{1,2},{2,1},{3,0},{4,7},{5,6},{6,5},{7,4},{8,11},{9,10},{10,... | collective-permute-start | bytes 98312 | tf_op jit(solution)/shard_map/ppermute | solution.py:129
  10.9 0.0 collective-permute-done.2.rest_2_
  10.9 0.5 %collective-permute-start.4 = (f32[64,256]{1,0:T(8,128)S(1)}, f32[64,256]{1,0:T(8,128)S(1)}, u32[]{:S(2)}, u32[]{:S(2)}) collective-permute-start(f32[64,256]{1,0:T(8,128)S(1)} %pad_maximum_fusion), channel_id=1, source_target_pairs={{0,1},{1,0},{2,3},{3,2},{4,5},{5,4},{6,7},{7,6},{8,9},{9,8},{10,11... | collective-permute-start | bytes 196616 | tf_op jit(solution)/shard_map/ppermute | solution.py:129
  11.4 1.9 %collective-permute-done.5.rest_1_ = f32[32,256]{1,0:T(8,128)S(1)} collective-permute-done((f32[32,256]{1,0:T(8,128)S(1)}, f32[32,256]{1,0:T(8,128)S(1)}, u32[]{:S(2)}, u32[]{:S(2)}) %collective-permute-start.5) | collective-permute-done | bytes 32800 | tf_op jit(solution)/shard_map/ppermute | solution.py:129
  13.3 0.4 %collective-permute-start.6 = (f32[32,256]{1,0:T(8,128)S(1)}, f32[32,256]{1,0:T(8,128)S(1)}, u32[]{:S(2)}, u32[]{:S(2)}) collective-permute-start(f32[32,256]{1,0:T(8,128)S(1)} %collective-permute-done.5.rest_1_), channel_id=1, source_target_pairs={{0,1},{1,0},{2,3},{3,2},{4,5},{5,4},{6,7},{7,6},{8,9},{9,8},{10,11... | collective-permute-start | bytes 98312 | tf_op jit(solution)/shard_map/ppermute | solution.py:129
  13.7 0.0 copy-done
  13.7 0.1 pad_maximum_fusion.3.params_ref
  13.7 0.5 %prepare.1 = (f32[8,256]{1,0:T(8,128)S(1)}, bf16[64,256]{1,0:T(8,128)(2,1)S(1)}, f32[8,256]{1,0:T(8,128)S(1)}, f32[8,256]{1,0:T(8,128)S(1)}) custom-call(f32[16,256]{1,0:T(8,128)S(1)} %pad_maximum_fusion.2.own_ref, f32[9]{0:T(128)S(1)} %pad_maximum_fusion.3.params_ref), custom_call_target="tpu_custom_call" | custom-call | flops 100000 | bytes 16384 | tf_op jit(solution)/shard_map/prepare/pallas_call | solution.py:163
  14.2 0.0 collective-permute-done.3.rest_3_
  14.2 1.0 %shard_map.46.acc_ref = f32[8,256]{1,0:T(8,128)S(1)} custom-call(f32[8,256]{1,0:T(8,128)S(1)} %get-tuple-element.9.scale_ref, bf16[64,256]{1,0:T(8,128)(2,1)S(1)} %get-tuple-element.10.side_ref, f32[8,256]{1,0:T(8,128)S(1)} %get-tuple-element.11.acc_ref, f32[16,256]{1,0:T(8,128)S(1)} %collective-permute-done.rest_0_, ...), custom_call_target="tpu_custom_call" | custom-call | flops 183500800 | bytes 114688 | tf_op jit(solution)/shard_map/pallas_call | solution.py:182
  15.3 0.0 collective-permute-done.4.rest_0_
  15.3 0.9 %shard_map.47.acc_ref = f32[8,256]{1,0:T(8,128)S(1)} custom-call(f32[8,256]{1,0:T(8,128)S(1)} %get-tuple-element.9.scale_ref, bf16[64,256]{1,0:T(8,128)(2,1)S(1)} %get-tuple-element.10.side_ref, f32[8,256]{1,0:T(8,128)S(1)} %shard_map.46.acc_ref, f32[64,256]{1,0:T(8,128)S(1)} %collective-permute-done.4.rest_0_, f32[32,256]{1,0:T(8,128)S(1)} %collective-permute-done.5.rest_1_), custom_call_target="tpu_custom_call" | custom-call | flops 157286400 | bytes 98304 | tf_op jit(solution)/shard_map/pallas_call | solution.py:182
  16.2 0.0 collective-permute-done.6.rest_1_
  16.2 1.1 %shard_map.48 = f32[8,256]{1,0:T(8,128)} custom-call(f32[8,256]{1,0:T(8,128)S(1)} %get-tuple-element.9.scale_ref, bf16[64,256]{1,0:T(8,128)(2,1)S(1)} %get-tuple-element.10.side_ref, f32[8,256]{1,0:T(8,128)S(1)} %shard_map.47.acc_ref, f32[8,256]{1,0:T(8,128)S(1)} %get-tuple-element.12.rest_0_, f32[32,256]{1,0:T(8,128)S(1)} %collective-permute-done.6.rest_1_), custom_call_target="tpu_custom_call" | custom-call | flops 52428800 | bytes 32768 | tf_op jit(solution)/shard_map/pallas_call | solution.py:182
  (2 shorter events, 0.0 us)
Async XLA Ops:
  0.7 4.9 %collective-permute-start = (f32[16,256]{1,0:T(8,128)S(1)}, f32[16,256]{1,0:T(8,128)S(1)}, u32[]{:S(2)}, u32[]{:S(2)}) collective-permute-start(f32[16,256]{1,0:T(8,128)S(1)} %pad_maximum_fusion.2.own_ref), channel_id=1, source_target_pairs={{0,9},{1,8},{2,11},{3,10},{4,13},{5,12},{6,15},{7,14},{8,1},{9,0},... | collective-permute-start | bytes 49160 | tf_op jit(solution)/shard_map/ppermute | solution.py:129
  5.7 4.3 %collective-permute-start.1 = (f32[32,256]{1,0:T(8,128)S(1)}, f32[32,256]{1,0:T(8,128)S(1)}, u32[]{:S(2)}, u32[]{:S(2)}) collective-permute-start(f32[32,256]{1,0:T(8,128)S(1)} %pad_maximum_fusion.1), channel_id=1, source_target_pairs={{0,5},{1,4},{2,7},{3,6},{4,1},{5,0},{6,3},{7,2},{8,13},{9,12},{10,... | collective-permute-start | bytes 98312 | tf_op jit(solution)/shard_map/ppermute | solution.py:129
  7.6 3.3 %collective-permute-start.2 = (f32[32,256]{1,0:T(8,128)S(1)}, f32[32,256]{1,0:T(8,128)S(1)}, u32[]{:S(2)}, u32[]{:S(2)}) collective-permute-start(f32[32,256]{1,0:T(8,128)S(1)} %pad_maximum_fusion.1), channel_id=1, source_target_pairs={{0,3},{1,2},{2,1},{3,0},{4,7},{5,6},{6,5},{7,4},{8,11},{9,10},{10,... | collective-permute-start | bytes 98312 | tf_op jit(solution)/shard_map/ppermute | solution.py:129
  9.7 3.9 %copy-start = (f32[8]{0:T(128)S(1)}, f32[8]{0:T(128)}, u32[]{:S(2)}) copy-start(f32[8]{0:T(128)} %param.6) | copy-start | bytes 100
  9.7 4.5 %collective-permute-start.3 = (f32[32,256]{1,0:T(8,128)S(1)}, f32[32,256]{1,0:T(8,128)S(1)}, u32[]{:S(2)}, u32[]{:S(2)}) collective-permute-start(f32[32,256]{1,0:T(8,128)S(1)} %pad_maximum_fusion.1), channel_id=1, source_target_pairs={{0,1},{1,0},{2,3},{3,2},{4,5},{5,4},{6,7},{7,6},{8,9},{9,8},{10,11... | collective-permute-start | bytes 98312 | tf_op jit(solution)/shard_map/ppermute | solution.py:129
  9.9 3.3 %collective-permute-start.5 = (f32[32,256]{1,0:T(8,128)S(1)}, f32[32,256]{1,0:T(8,128)S(1)}, u32[]{:S(2)}, u32[]{:S(2)}) collective-permute-start(f32[32,256]{1,0:T(8,128)S(1)} %collective-permute-done.1.rest_1_), channel_id=1, source_target_pairs={{0,3},{1,2},{2,1},{3,0},{4,7},{5,6},{6,5},{7,4},{8,11},{9,10},{10,... | collective-permute-start | bytes 98312 | tf_op jit(solution)/shard_map/ppermute | solution.py:129
  10.9 4.4 %collective-permute-start.4 = (f32[64,256]{1,0:T(8,128)S(1)}, f32[64,256]{1,0:T(8,128)S(1)}, u32[]{:S(2)}, u32[]{:S(2)}) collective-permute-start(f32[64,256]{1,0:T(8,128)S(1)} %pad_maximum_fusion), channel_id=1, source_target_pairs={{0,1},{1,0},{2,3},{3,2},{4,5},{5,4},{6,7},{7,6},{8,9},{9,8},{10,11... | collective-permute-start | bytes 196616 | tf_op jit(solution)/shard_map/ppermute | solution.py:129
  13.3 3.0 %collective-permute-start.6 = (f32[32,256]{1,0:T(8,128)S(1)}, f32[32,256]{1,0:T(8,128)S(1)}, u32[]{:S(2)}, u32[]{:S(2)}) collective-permute-start(f32[32,256]{1,0:T(8,128)S(1)} %collective-permute-done.5.rest_1_), channel_id=1, source_target_pairs={{0,1},{1,0},{2,3},{3,2},{4,5},{5,4},{6,7},{7,6},{8,9},{9,8},{10,11... | collective-permute-start | bytes 98312 | tf_op jit(solution)/shard_map/ppermute | solution.py:129
